TPU v7x, 32 devices: a whole 2x2x4 slice. The times are simulated.
32 devices in a mesh: cp: 4 (over z), fsdp: 8 (over y, x, core).
Axes of the slice: x: 2, y: 2, z: 4, core: 2. Of those that a mesh axis runs over, the one named last changes fastest.
Arguments:
- hidden: bfloat16 [128, 512, 2048], P('fsdp', 'cp')
- tok_pos: int32 [128, 512], P('fsdp', 'cp')
- grad_out: bfloat16 [128, 512, 2048], P('fsdp', 'cp')
- norm_gain: float32 [2048], P(('fsdp', 'cp'))
- w_query: bfloat16 [2048, 2048], P(('fsdp', 'cp'))
- w_key: bfloat16 [2048, 256], P(('fsdp', 'cp'))
- w_value: bfloat16 [2048, 256], P(('fsdp', 'cp'))
- w_out: bfloat16 [2048, 2048], P(('fsdp', 'cp'))
Outputs:
- output 1: bfloat16 [128, 512, 2048], P('fsdp', 'cp')
- output 2: bfloat16 [128, 512, 2048], P('fsdp', 'cp')
- output 3: float32 [2048, 2048], P(('fsdp', 'cp'))
- output 4: float32 [2048, 256], P(('fsdp', 'cp'))
- output 5: float32 [2048, 256], P(('fsdp', 'cp'))
- output 6: float32 [2048, 2048], P(('fsdp', 'cp'))
- output 7: float32 [2048], P(('fsdp', 'cp'))
All inputs are finite; a program needn't handle non-finite values.
Results may differ from a plain program's by a relative error of at most 0.00769182.
Values are sent between devices in bfloat16 or wider.
A program may use at most 1 GiB of HBM per device.

v0:
```python
import jax
import jax.numpy as jnp
from jax import lax
from jax.sharding import PartitionSpec as P, NamedSharding

HEAD_DIM = 128
ROPE_THETA = 1000000.0
RMS_EPS = 1e-5
NEG_BIG = -1e30
SCALE = HEAD_DIM ** -0.5
TOKEN_DIMS = (((0,), (0,)), ((), ()))
LAST_DIMS = (((2,), (1,)), ((), ()))
ALL_AXES = ('fsdp', 'cp')


def rope_tables(positions):
    half_dim = HEAD_DIM // 2
    inv_freq = ROPE_THETA ** (-jnp.arange(half_dim, dtype=jnp.float32) / half_dim)
    angles = positions.astype(jnp.float32)[..., None] * inv_freq
    return jnp.cos(angles)[..., None, :], jnp.sin(angles)[..., None, :]


def rope_apply(values, cos_tab, sin_tab):
    half_dim = HEAD_DIM // 2
    first_half = values[..., :half_dim]
    second_half = values[..., half_dim:]
    return jnp.concatenate([first_half * cos_tab - second_half * sin_tab, second_half * cos_tab + first_half * sin_tab], axis=-1)


def rope_transpose(values, cos_tab, sin_tab):
    half_dim = HEAD_DIM // 2
    first_half = values[..., :half_dim]
    second_half = values[..., half_dim:]
    return jnp.concatenate([first_half * cos_tab + second_half * sin_tab, second_half * cos_tab - first_half * sin_tab], axis=-1)


def norm_project(hidden, tok_pos, gain_full, wq_full, wk_full, wv_full):
    n_seq, n_rows, _ = hidden.shape
    num_heads = wq_full.shape[1] // HEAD_DIM
    kv_heads = wk_full.shape[1] // HEAD_DIM
    x_f32 = hidden.astype(jnp.float32)
    inv_rms = lax.rsqrt(jnp.mean(x_f32 * x_f32, axis=-1) + RMS_EPS)
    x_hat = x_f32 * inv_rms[..., None]
    normed = (x_hat * gain_full).astype(jnp.bfloat16)
    cos_tab, sin_tab = rope_tables(tok_pos)
    q_lin = jnp.dot(normed, wq_full, preferred_element_type=jnp.float32).reshape(n_seq, n_rows, num_heads, HEAD_DIM)
    k_lin = jnp.dot(normed, wk_full, preferred_element_type=jnp.float32).reshape(n_seq, n_rows, kv_heads, HEAD_DIM)
    q_grp = rope_apply(q_lin, cos_tab, sin_tab).astype(jnp.bfloat16).reshape(n_seq, n_rows, kv_heads, num_heads // kv_heads, HEAD_DIM)
    k_rot = rope_apply(k_lin, cos_tab, sin_tab).astype(jnp.bfloat16)
    v_val = jnp.dot(normed, wv_full, preferred_element_type=jnp.float32).astype(jnp.bfloat16).reshape(n_seq, n_rows, kv_heads, HEAD_DIM)
    return x_f32, inv_rms, x_hat, normed, cos_tab, sin_tab, q_grp, k_rot, v_val


def attn_fwd_block(q_grp, k_blk, v_blk, q_pos, key_pos, run_stats):
    row_max, row_sum, out_acc = run_stats
    scores = jnp.einsum('bikgd,bjkd->bkigj', q_grp, k_blk, preferred_element_type=jnp.float32) * SCALE
    visible = key_pos[:, None, None, None, :] <= q_pos[:, None, :, None, None]
    scores = jnp.where(visible, scores, NEG_BIG)
    new_max = jnp.maximum(row_max, jnp.max(scores, axis=-1))
    att_probs = jnp.where(visible, jnp.exp(scores - new_max[..., None]), 0.0)
    rescale = jnp.exp(row_max - new_max)
    row_sum = row_sum * rescale + jnp.sum(att_probs, axis=-1)
    out_acc = out_acc * rescale[..., None] + jnp.einsum('bkigj,bjkd->bkigd', att_probs.astype(jnp.bfloat16), v_blk, preferred_element_type=jnp.float32)
    return new_max, row_sum, out_acc


def attn_bwd_block(q_grp, k_blk, v_blk, gout_grp, log_sum, row_delta, q_pos, key_pos):
    scores = jnp.einsum('bikgd,bjkd->bkigj', q_grp, k_blk, preferred_element_type=jnp.float32) * SCALE
    visible = key_pos[:, None, None, None, :] <= q_pos[:, None, :, None, None]
    att_probs = jnp.where(visible, jnp.exp(scores - log_sum[..., None]), 0.0)
    grad_v = jnp.einsum('bkigj,bikgd->bkjd', att_probs.astype(jnp.bfloat16), gout_grp, preferred_element_type=jnp.float32)
    grad_probs = jnp.einsum('bikgd,bjkd->bkigj', gout_grp, v_blk, preferred_element_type=jnp.float32)
    grad_scores = (att_probs * (grad_probs - row_delta[..., None])).astype(jnp.bfloat16)
    grad_q = jnp.einsum('bkigj,bjkd->bkigd', grad_scores, k_blk, preferred_element_type=jnp.float32)
    grad_k = jnp.einsum('bkigj,bikgd->bkjd', grad_scores, q_grp, preferred_element_type=jnp.float32)
    return grad_q, grad_k, grad_v


def attn_output(run_stats):
    row_max, row_sum, out_acc = run_stats
    n_seq, _, n_rows, _ = row_sum.shape
    attn_flat = jnp.transpose((out_acc / row_sum[..., None]).astype(jnp.bfloat16), (0, 2, 1, 3, 4)).reshape(n_seq, n_rows, -1)
    return attn_flat, row_max + jnp.log(row_sum)


def finish_backward(grad_q, grad_k, grad_v, fwd_saved, grad_out, gain_full, wq_full, wk_full, wv_full):
    inv_rms, x_hat, normed, cos_tab, sin_tab = fwd_saved
    n_seq, n_rows, model_dim = normed.shape
    tokens = n_seq * n_rows
    q_rows = jnp.transpose(grad_q * SCALE, (0, 2, 1, 3, 4)).reshape(n_seq, n_rows, -1, HEAD_DIM)
    dq_pre = rope_transpose(q_rows, cos_tab, sin_tab).astype(jnp.bfloat16).reshape(n_seq, n_rows, -1)
    dk_pre = rope_transpose(jnp.transpose(grad_k * SCALE, (0, 2, 1, 3)), cos_tab, sin_tab).astype(jnp.bfloat16).reshape(n_seq, n_rows, -1)
    dv_pre = jnp.transpose(grad_v, (0, 2, 1, 3)).astype(jnp.bfloat16).reshape(n_seq, n_rows, -1)
    normed_flat = normed.reshape(tokens, model_dim)
    grad_wq = lax.dot_general(normed_flat, dq_pre.reshape(tokens, -1), TOKEN_DIMS, preferred_element_type=jnp.float32)
    grad_wk = lax.dot_general(normed_flat, dk_pre.reshape(tokens, -1), TOKEN_DIMS, preferred_element_type=jnp.float32)
    grad_wv = lax.dot_general(normed_flat, dv_pre.reshape(tokens, -1), TOKEN_DIMS, preferred_element_type=jnp.float32)
    grad_normed = (lax.dot_general(dq_pre, wq_full, LAST_DIMS, preferred_element_type=jnp.float32) + lax.dot_general(dk_pre, wk_full, LAST_DIMS, preferred_element_type=jnp.float32) + lax.dot_general(dv_pre, wv_full, LAST_DIMS, preferred_element_type=jnp.float32))
    value_a9 = grad_normed * gain_full
    grad_gain = jnp.sum(grad_normed * x_hat, axis=(0, 1))
    grad_x = inv_rms[..., None] * (value_a9 - x_hat * jnp.mean(value_a9 * x_hat, axis=-1, keepdims=True))
    grad_hidden = (grad_out.astype(jnp.float32) + grad_x).astype(jnp.bfloat16)
    return grad_hidden, grad_wq, grad_wk, grad_wv, grad_gain


def solution(mesh):
    cp_size = mesh.shape['cp']
    shift_perm = [(src_idx, (src_idx + 1) % cp_size) for src_idx in range(cp_size)]

    def pass_on(local_part):
        return lax.ppermute(local_part, 'cp', shift_perm)

    def collect_full(local_part):
        return lax.all_gather(local_part, ALL_AXES, axis=0, tiled=True)

    def sum_to_shards(part_sum):
        return lax.psum_scatter(part_sum, ALL_AXES, scatter_dimension=0, tiled=True)

    def shard_fn(hidden, tok_pos, grad_out, norm_gain, w_query, w_key, w_value, w_out):
        gain_full = collect_full(norm_gain)
        x_f32, inv_rms, x_hat, normed, cos_tab, sin_tab, q_grp, k_rot, v_val = norm_project(hidden, tok_pos, gain_full, collect_full(w_query), collect_full(w_key), collect_full(w_value))
        n_seq, n_rows, kv_heads, group_size, _ = q_grp.shape
        stat_shape = (n_seq, kv_heads, n_rows, group_size)
        init_stats = (jnp.full(stat_shape, NEG_BIG, jnp.float32), jnp.zeros(stat_shape, jnp.float32), jnp.zeros(stat_shape + (HEAD_DIM,), jnp.float32))
        own_stats = attn_fwd_block(q_grp, k_rot, v_val, tok_pos, tok_pos, init_stats)

        def fwd_step(step_idx, loop_carry):
            k_blk, v_blk, key_pos, run_stats = loop_carry
            k_blk = pass_on(k_blk)
            v_blk = pass_on(v_blk)
            key_pos = pass_on(key_pos)
            return k_blk, v_blk, key_pos, attn_fwd_block(q_grp, k_blk, v_blk, tok_pos, key_pos, run_stats)

        run_stats = lax.fori_loop(1, cp_size, fwd_step, (k_rot, v_val, tok_pos, own_stats))[3]
        attn_flat, log_sum = attn_output(run_stats)
        result = (x_f32 + jnp.dot(attn_flat, collect_full(w_out), preferred_element_type=jnp.float32)).astype(jnp.bfloat16)

        tokens = n_seq * n_rows
        grad_wo = lax.dot_general(attn_flat.reshape(tokens, -1), grad_out.reshape(tokens, -1), TOKEN_DIMS, preferred_element_type=jnp.float32)
        gout_grp = lax.dot_general(grad_out, collect_full(w_out), LAST_DIMS, preferred_element_type=jnp.float32).astype(jnp.bfloat16).reshape(q_grp.shape)
        row_delta = jnp.einsum('bikgd,bikgd->bkig', gout_grp, attn_flat.reshape(q_grp.shape), preferred_element_type=jnp.float32)
        own_grads = attn_bwd_block(q_grp, k_rot, v_val, gout_grp, log_sum, row_delta, tok_pos, tok_pos)

        def bwd_step(step_idx, loop_carry):
            k_blk, v_blk, key_pos, grad_q, grad_k, grad_v = loop_carry
            k_blk = pass_on(k_blk)
            v_blk = pass_on(v_blk)
            key_pos = pass_on(key_pos)
            grad_k = pass_on(grad_k)
            grad_v = pass_on(grad_v)
            part_q, part_k, part_v = attn_bwd_block(q_grp, k_blk, v_blk, gout_grp, log_sum, row_delta, tok_pos, key_pos)
            return k_blk, v_blk, key_pos, grad_q + part_q, grad_k + part_k, grad_v + part_v

        loop_out = lax.fori_loop(1, cp_size, bwd_step, (k_rot, v_val, tok_pos) + own_grads)
        grad_k = pass_on(loop_out[4])
        grad_v = pass_on(loop_out[5])
        fwd_saved = (inv_rms, x_hat, normed, cos_tab, sin_tab)
        grad_hidden, grad_wq, grad_wk, grad_wv, grad_gain = finish_backward(loop_out[3], grad_k, grad_v, fwd_saved, grad_out, gain_full, collect_full(w_query), collect_full(w_key), collect_full(w_value))
        return (result, grad_hidden, sum_to_shards(grad_wq), sum_to_shards(grad_wk), sum_to_shards(grad_wv), sum_to_shards(grad_wo), sum_to_shards(grad_gain))

    row_spec = P('fsdp', 'cp', None)
    pos_spec = P('fsdp', 'cp')
    weight_spec = P(ALL_AXES, None)
    gain_spec = P(ALL_AXES)
    return jax.shard_map(shard_fn, mesh=mesh, in_specs=(row_spec, pos_spec, row_spec, gain_spec, weight_spec, weight_spec, weight_spec, weight_spec), out_specs=(row_spec, row_spec, weight_spec, weight_spec, weight_spec, weight_spec, gain_spec), check_vma=False)
```

profile of v0, /device:TPU:0, one launch (start us, length us, event | category | flops | bytes accessed | tf_op | source)
XLA Modules:
  0.0 2191.7 jit_solution(5620667459202514791)
XLA Ops:
  16.2 42.1 %all-reduce = f32[2048]{0:T(1024)S(1)} all-reduce(f32[2048]{0:T(1024)S(1)} %dynamic-update-slice), channel_id=1, replica_groups=mesh['cp'=4,'fsdp'=8] {'fsdp','cp'}, use_global_device_ids=true, to_apply=%add | all-reduce | flops 2048 | bytes 16384
  87.7 35.8 %all-gather.7.cloned.1.call-done = bf16[2048,256]{1,0:T(8,128)(2,1)} async-done(((bf16[64,256]{1,0:T(8,128)(2,1)}), bf16[2048,256]{1,0:T(8,128)(2,1)}) %all-gather.7.cloned.1.call-update) | async-done | bytes 1048592 | tf_op jit(solution)/shard_map/all_gather | solution.py:114
  142.6 59.8 %all-gather.9.cloned.1.call-done = bf16[2048,2048]{1,0:T(8,128)(2,1)} async-done(((bf16[64,2048]{1,0:T(8,128)(2,1)}), bf16[2048,2048]{1,0:T(8,128)(2,1)}) %all-gather.9.cloned.1.call-update) | async-done | bytes 8388624 | tf_op jit(solution)/shard_map/all_gather | solution.py:114
  202.5 24.2 %fusion.58 = f32[16,128,2048]{2,1,0:T(8,128)} fusion(bf16[16,128,2048]{2,1,0:T(8,128)(2,1)} %fusion.34, bf16[2048,2048]{1,0:T(8,128)(2,1)} %all-gather.9.cloned.1.call-done), kind=kOutput, calls=%fused_computation.81 | convolution fusion | flops 17179869184 | bytes 33554432 | tf_op jit(solution)/shard_map/dot_general | solution.py:46
  297.0 23.8 %fusion.69 = bf16[16,128,2048]{2,1,0:T(8,128)(2,1)} fusion(bf16[16,128,2048]{2,1,0:T(8,128)(2,1)} %param.14, bf16[2048,2048]{1,0:T(8,128)(2,1)} %all-gather.11.cloned.1.call-done), kind=kOutput, calls=%fused_computation.94 | convolution fusion | flops 17184063488 | bytes 25165824 | tf_op jit(solution)/shard_map/dot_general | solution.py:140
  341.8 15.9 convolution_add_fusion.1
  357.8 216.8 %while.40 = (s32[]{:T(128)}, bf16[16,128,2,128]{3,1,2,0:T(8,128)(2,1)}, bf16[16,128,2,128]{3,1,2,0:T(8,128)(2,1)}, s32[16,128]{1,0:T(8,128)}, f32[16,2,128,8]{2,...) while((s32[]{:T(128)}, ...), condition=%wide.region_6.7_spmd, body=%wide.region_3.6_spmd.sunk | while | flops 2210725888 | bytes 178323776 | solution.py:134
  362.0 24.2 %collective-permute-done.2 = s32[16,128]{1,0:T(8,128)S(1)} collective-permute-done((s32[16,128]{1,0:T(8,128)}, s32[16,128]{1,0:T(8,128)S(1)}, u32[]{:S(2)}, u32[]{:S(2)}) %collective-permute-start.2) | collective-permute-done | bytes 8224 | tf_op jit(solution)/shard_map/while/body/eval_jaxpr/ppermute | solution.py:111
  412.9 17.3 multiply_add_fusion.7
  432.4 26.0 %collective-permute-done.2 = s32[16,128]{1,0:T(8,128)S(1)} collective-permute-done((s32[16,128]{1,0:T(8,128)}, s32[16,128]{1,0:T(8,128)S(1)}, u32[]{:S(2)}, u32[]{:S(2)}) %collective-permute-start.2) | collective-permute-done | bytes 8224 | tf_op jit(solution)/shard_map/while/body/eval_jaxpr/ppermute | solution.py:111
  485.1 17.3 multiply_add_fusion.7
  503.1 27.5 %collective-permute-done.2 = s32[16,128]{1,0:T(8,128)S(1)} collective-permute-done((s32[16,128]{1,0:T(8,128)}, s32[16,128]{1,0:T(8,128)S(1)}, u32[]{:S(2)}, u32[]{:S(2)}) %collective-permute-start.2) | collective-permute-done | bytes 8224 | tf_op jit(solution)/shard_map/while/body/eval_jaxpr/ppermute | solution.py:111
  557.3 17.3 multiply_add_fusion.7
  588.2 17.6 copy.74
  605.9 17.6 copy.112
  623.5 16.1 multiply_reduce_fusion
  639.6 14.1 multiply_convert_fusion.1
  684.0 430.1 %while.41 = (s32[]{:T(128)}, bf16[16,128,2,128]{3,1,2,0:T(8,128)(2,1)S(1)}, bf16[16,128,2,128]{3,1,2,0:T(8,128)(2,1)}, s32[16,128]{1,0:T(8,128)S(1)}, f32[16,2,1...) while((s32[]{:T(128)}, ...), condition=%wide.region_8.9_spmd, body=%wide.region_7.8_spmd.sunk | while | flops 5416157184 | bytes 259228208 | solution.py:154
  689.3 23.0 %collective-permute-done.5 = s32[16,128]{1,0:T(8,128)S(1)} collective-permute-done((s32[16,128]{1,0:T(8,128)S(1)}, s32[16,128]{1,0:T(8,128)S(1)}, u32[]{:S(2)}, u32[]{:S(2)}) %collective-permute-start.5) | collective-permute-done | bytes 8224 | tf_op jit(solution)/shard_map/while/body/eval_jaxpr/ppermute | solution.py:111
  718.7 16.1 collective-permute-done.4
  750.4 16.3 convolution_add_fusion.3
  766.7 13.1 collective-permute-done.6
  790.0 24.0 %collective-permute-done.7 = f32[16,2,128,128]{3,2,1,0:T(8,128)} collective-permute-done((f32[16,2,128,128]{3,2,1,0:T(8,128)}, f32[16,2,128,128]{3,2,1,0:T(8,128)}, u32[]{:S(2)}, u32[]{:S(2)}) %collective-permute-start.7) | collective-permute-done | bytes 2097184 | tf_op jit(solution)/shard_map/while/body/eval_jaxpr/ppermute | solution.py:111
  814.0 14.3 bitcast_add_fusion.5
  833.4 23.0 %collective-permute-done.5 = s32[16,128]{1,0:T(8,128)S(1)} collective-permute-done((s32[16,128]{1,0:T(8,128)S(1)}, s32[16,128]{1,0:T(8,128)S(1)}, u32[]{:S(2)}, u32[]{:S(2)}) %collective-permute-start.5) | collective-permute-done | bytes 8224 | tf_op jit(solution)/shard_map/while/body/eval_jaxpr/ppermute | solution.py:111
  862.9 16.1 collective-permute-done.4
  894.6 16.3 convolution_add_fusion.3
  934.2 23.1 %collective-permute-done.7 = f32[16,2,128,128]{3,2,1,0:T(8,128)} collective-permute-done((f32[16,2,128,128]{3,2,1,0:T(8,128)}, f32[16,2,128,128]{3,2,1,0:T(8,128)}, u32[]{:S(2)}, u32[]{:S(2)}) %collective-permute-start.7) | collective-permute-done | bytes 2097184 | tf_op jit(solution)/shard_map/while/body/eval_jaxpr/ppermute | solution.py:111
  957.3 14.3 bitcast_add_fusion.5
  976.8 23.0 %collective-permute-done.5 = s32[16,128]{1,0:T(8,128)S(1)} collective-permute-done((s32[16,128]{1,0:T(8,128)S(1)}, s32[16,128]{1,0:T(8,128)S(1)}, u32[]{:S(2)}, u32[]{:S(2)}) %collective-permute-start.5) | collective-permute-done | bytes 8224 | tf_op jit(solution)/shard_map/while/body/eval_jaxpr/ppermute | solution.py:111
  1006.2 16.1 collective-permute-done.4
  1037.9 16.3 convolution_add_fusion.3
  1077.5 22.2 %collective-permute-done.7 = f32[16,2,128,128]{3,2,1,0:T(8,128)} collective-permute-done((f32[16,2,128,128]{3,2,1,0:T(8,128)}, f32[16,2,128,128]{3,2,1,0:T(8,128)}, u32[]{:S(2)}, u32[]{:S(2)}) %collective-permute-start.7) | collective-permute-done | bytes 2097184 | tf_op jit(solution)/shard_map/while/body/eval_jaxpr/ppermute | solution.py:111
  1099.8 14.3 bitcast_add_fusion.5
  1114.2 17.8 copy.83
  1144.7 29.1 %collective-permute-done.9 = bf16[16,2,128,128]{3,2,1,0:T(8,128)(2,1)S(1)} collective-permute-done((bf16[16,2,128,128]{3,2,1,0:T(8,128)(2,1)S(1)}, bf16[16,2,128,128]{3,2,1,0:T(8,128)(2,1)S(1)}, u32[]{:S(2)}, u32[]{:S(2)}) %collective-permute-start.9) | collective-permute-done | bytes 1048608 | tf_op jit(solution)/shard_map/ppermute | solution.py:111
  1218.8 17.5 multiply_add_fusion.2
  1259.9 22.1 %fusion.49 = f32[2048,2048]{1,0:T(8,128)} fusion(bf16[2048,2048]{1,0:T(8,128)(2,1)} %bitcast.208, bf16[256,8,16,128]{3,2,1,0:T(8,128)(2,1)S(1)} %bitcast.201), kind=kOutput, calls=%fused_computation.71 | convolution fusion | flops 17179869184 | bytes 33554432 | tf_op jit(solution)/shard_map/dot_general | solution.py:95
  1294.9 13.3 reshape_reshape.9
  1308.3 24.4 %fusion.108 = f32[2048,2048]{1,0:T(8,128)} fusion(bf16[2048,2048]{1,0:T(8,128)(2,1)} %reshape_reshape.9, bf16[2048,2048]{1,0:T(8,128)(2,1)} %bitcast.210), kind=kOutput, calls=%fused_computation.148 | convolution fusion | flops 17179869184 | bytes 33554432 | tf_op jit(solution)/shard_map/dot_general | solution.py:139
  1333.3 13.3 convert_element_type.100
  1346.7 24.5 %fusion.42 = bf16[16,128,2048]{2,1,0:T(8,128)(2,1)} fusion(bf16[16,128,2048]{2,1,0:T(8,128)(2,1)} %param.12, bf16[16,128,2048]{1,2,0:T(8,128)(2,1)} %bitcast.200, bf16[2048,2048]{1,0:T(8,128)(2,1)} %all-gather.11.cloned.1.call-done), kind=kOutput, calls=%fused_computation.53 | convolution fusion | flops 17192452096 | bytes 33554432 | tf_op jit(solution)/shard_map/dot_general | solution.py:136
  1371.2 23.2 %fusion.56 = f32[16,128,2048]{2,1,0:T(8,128)} fusion(bf16[16,128,2048]{2,1,0:T(8,128)(2,1)S(1)} %copy-done.15, bf16[2048,2048]{1,0:T(8,128)(2,1)} %all-gather.9.cloned.1.call-done), kind=kOutput, calls=%fused_computation.79 | convolution fusion | flops 17179869184 | bytes 33554432 | tf_op jit(solution)/shard_map/dot_general | solution.py:98
  1397.6 15.8 fusion.40
  1413.4 37.2 %all-reduce.1 = f32[2048]{0:T(1024)S(1)} all-reduce(f32[2048]{0:T(1024)S(1)} %get-tuple-element.189), channel_id=6, replica_groups=mesh['cp'=4,'fsdp'=8] {'fsdp','cp'}, use_global_device_ids=true, to_apply=%region_15.16.clone | all-reduce | flops 2048 | bytes 16384
  1451.2 14.9 fusion.39
  1466.1 353.6 %reduce-scatter.5.cloned.1.call-done = f32[64,2048]{1,0:T(8,128)} async-done(((f32[2048,2048]{1,0:T(8,128)}), f32[64,2048]{1,0:T(8,128)}) %reduce-scatter.5.cloned.1.call-update) | async-done | bytes 524304 | tf_op jit(solution)/shard_map/reduce_scatter | solution.py:117
  1819.7 364.8 %reduce-scatter.11.cloned.1.call-done = f32[64,2048]{1,0:T(8,128)} async-done(((f32[2048,2048]{1,0:T(8,128)}), f32[64,2048]{1,0:T(8,128)}) %reduce-scatter.11.cloned.1.call-update) | async-done | bytes 524304 | tf_op jit(solution)/shard_map/reduce_scatter | solution.py:117
  (286 shorter events, 514.4 us)
Async XLA Ops:
  7.2 56.3 %copy-start.24 = (s32[16,128]{1,0:T(8,128)S(1)}, s32[16,128]{1,0:T(8,128)}, u32[]{:S(2)}) copy-start(s32[16,128]{1,0:T(8,128)} %param.13) | copy-start | bytes 24580
  7.2 69.7 %all-gather.5.cloned.1.call-start = ((), (), s32[]{:S(2)}) async-start(), calls=%async_computation.4 | async-start | bytes 1081344 | tf_op jit(solution)/shard_map/all_gather | solution.py:114
  7.9 115.6 %all-gather.7.cloned.1.call-start = ((), (), s32[]{:S(2)}) async-start(), calls=%async_computation.5 | async-start | bytes 1081344 | tf_op jit(solution)/shard_map/all_gather | solution.py:114
  8.7 193.8 %all-gather.9.cloned.1.call-start = ((), (), s32[]{:S(2)}) async-start(), calls=%async_computation.6 | async-start | bytes 8650752 | tf_op jit(solution)/shard_map/all_gather | solution.py:114
  9.4 287.6 %all-gather.11.cloned.1.call-start = ((), (), s32[]{:S(2)}) async-start(), calls=%async_computation.7 | async-start | bytes 8650752 | tf_op jit(solution)/shard_map/all_gather | solution.py:114
  10.0 1456.1 %reduce-scatter.9.cloned.1.call-start = ((), (), s32[]{:S(2)}) async-start(), calls=%async_computation.10 | async-start | bytes 2162688 | tf_op jit(solution)/shard_map/reduce_scatter | solution.py:117
  63.8 211.2 %copy-start.20 = (pred[16,128,128]{1,2,0:T(8,128)(4,1)}, pred[16,128,128]{1,2,0:T(8,128)(4,1)S(1)}, u32[]{:S(2)}) copy-start(pred[16,128,128]{1,2,0:T(8,128)(4,1)S(1)} %broadcast_compare_fusion.2) | copy-start | bytes 786436
  67.5 168.6 %copy-start.3 = (f32[16,128,64]{2,1,0:T(8,128)}, f32[16,128,64]{2,1,0:T(8,128)S(1)}, u32[]{:S(2)}) copy-start(f32[16,128,64]{2,1,0:T(8,128)S(1)} %get-tuple-element.253) | copy-start | bytes 1572868
  67.5 168.6 %copy-start.5 = (f32[16,128,64]{2,1,0:T(8,128)}, f32[16,128,64]{2,1,0:T(8,128)S(1)}, u32[]{:S(2)}) copy-start(f32[16,128,64]{2,1,0:T(8,128)S(1)} %get-tuple-element.254) | copy-start | bytes 1572868
  136.8 138.2 %copy-start.7 = (bf16[16,128,2,128]{3,1,2,0:T(8,128)(2,1)}, bf16[16,128,2,128]{3,1,2,0:T(8,128)(2,1)S(1)}, u32[]{:S(2)}) copy-start(bf16[16,128,2,128]{3,1,2,0:T(8,128)(2,1)S(1)} %pad_maximum_fusion.1) | copy-start | bytes 3145732
  358.0 29.2 %collective-permute-start = (bf16[16,128,2,128]{3,1,2,0:T(8,128)(2,1)}, bf16[16,128,2,128]{3,1,2,0:T(8,128)(2,1)S(1)}, u32[]{:S(2)}, u32[]{:S(2)}) collective-permute-start(bf16[16,128,2,128]{3,1,2,0:T(8,128)(2,1)} %get-tuple-element.407), channel_id=1, source_target_pairs={{0,8},{8,16},{16,24},{24,0},{1,9},{9,17},{17,25},{25,1},{2,10},{10... | collective-permute-start | bytes 3145736 | tf_op jit(solution)/shard_map/while/body/eval_jaxpr/ppermute | solution.py:111
  359.8 26.4 %collective-permute-start.2 = (s32[16,128]{1,0:T(8,128)}, s32[16,128]{1,0:T(8,128)S(1)}, u32[]{:S(2)}, u32[]{:S(2)}) collective-permute-start(s32[16,128]{1,0:T(8,128)} %get-tuple-element.409), channel_id=1, source_target_pairs={{0,8},{8,16},{16,24},{24,0},{1,9},{9,17},{17,25},{25,1},{2,10},{10... | collective-permute-start | bytes 24584 | tf_op jit(solution)/shard_map/while/body/eval_jaxpr/ppermute | solution.py:111
  361.2 50.7 %collective-permute-start.1 = (bf16[16,128,2,128]{3,1,2,0:T(8,128)(2,1)}, bf16[16,128,2,128]{3,1,2,0:T(8,128)(2,1)S(1)}, u32[]{:S(2)}, u32[]{:S(2)}) collective-permute-start(bf16[16,128,2,128]{3,1,2,0:T(8,128)(2,1)} %get-tuple-element.408), channel_id=1, source_target_pairs={{0,8},{8,16},{16,24},{24,0},{1,9},{9,17},{17,25},{25,1},{2,10},{10... | collective-permute-start | bytes 3145736 | tf_op jit(solution)/shard_map/while/body/eval_jaxpr/ppermute | solution.py:111
  430.2 29.2 %collective-permute-start = (bf16[16,128,2,128]{3,1,2,0:T(8,128)(2,1)}, bf16[16,128,2,128]{3,1,2,0:T(8,128)(2,1)S(1)}, u32[]{:S(2)}, u32[]{:S(2)}) collective-permute-start(bf16[16,128,2,128]{3,1,2,0:T(8,128)(2,1)} %get-tuple-element.407), channel_id=1, source_target_pairs={{0,8},{8,16},{16,24},{24,0},{1,9},{9,17},{17,25},{25,1},{2,10},{10... | collective-permute-start | bytes 3145736 | tf_op jit(solution)/shard_map/while/body/eval_jaxpr/ppermute | solution.py:111
  430.2 28.2 %collective-permute-start.2 = (s32[16,128]{1,0:T(8,128)}, s32[16,128]{1,0:T(8,128)S(1)}, u32[]{:S(2)}, u32[]{:S(2)}) collective-permute-start(s32[16,128]{1,0:T(8,128)} %get-tuple-element.409), channel_id=1, source_target_pairs={{0,8},{8,16},{16,24},{24,0},{1,9},{9,17},{17,25},{25,1},{2,10},{10... | collective-permute-start | bytes 24584 | tf_op jit(solution)/shard_map/while/body/eval_jaxpr/ppermute | solution.py:111
  431.6 52.5 %collective-permute-start.1 = (bf16[16,128,2,128]{3,1,2,0:T(8,128)(2,1)}, bf16[16,128,2,128]{3,1,2,0:T(8,128)(2,1)S(1)}, u32[]{:S(2)}, u32[]{:S(2)}) collective-permute-start(bf16[16,128,2,128]{3,1,2,0:T(8,128)(2,1)} %get-tuple-element.408), channel_id=1, source_target_pairs={{0,8},{8,16},{16,24},{24,0},{1,9},{9,17},{17,25},{25,1},{2,10},{10... | collective-permute-start | bytes 3145736 | tf_op jit(solution)/shard_map/while/body/eval_jaxpr/ppermute | solution.py:111
  502.4 29.2 %collective-permute-start = (bf16[16,128,2,128]{3,1,2,0:T(8,128)(2,1)}, bf16[16,128,2,128]{3,1,2,0:T(8,128)(2,1)S(1)}, u32[]{:S(2)}, u32[]{:S(2)}) collective-permute-start(bf16[16,128,2,128]{3,1,2,0:T(8,128)(2,1)} %get-tuple-element.407), channel_id=1, source_target_pairs={{0,8},{8,16},{16,24},{24,0},{1,9},{9,17},{17,25},{25,1},{2,10},{10... | collective-permute-start | bytes 3145736 | tf_op jit(solution)/shard_map/while/body/eval_jaxpr/ppermute | solution.py:111
  502.4 28.2 %collective-permute-start.2 = (s32[16,128]{1,0:T(8,128)}, s32[16,128]{1,0:T(8,128)S(1)}, u32[]{:S(2)}, u32[]{:S(2)}) collective-permute-start(s32[16,128]{1,0:T(8,128)} %get-tuple-element.409), channel_id=1, source_target_pairs={{0,8},{8,16},{16,24},{24,0},{1,9},{9,17},{17,25},{25,1},{2,10},{10... | collective-permute-start | bytes 24584 | tf_op jit(solution)/shard_map/while/body/eval_jaxpr/ppermute | solution.py:111
  502.4 53.8 %collective-permute-start.1 = (bf16[16,128,2,128]{3,1,2,0:T(8,128)(2,1)}, bf16[16,128,2,128]{3,1,2,0:T(8,128)(2,1)S(1)}, u32[]{:S(2)}, u32[]{:S(2)}) collective-permute-start(bf16[16,128,2,128]{3,1,2,0:T(8,128)(2,1)} %get-tuple-element.408), channel_id=1, source_target_pairs={{0,8},{8,16},{16,24},{24,0},{1,9},{9,17},{17,25},{25,1},{2,10},{10... | collective-permute-start | bytes 3145736 | tf_op jit(solution)/shard_map/while/body/eval_jaxpr/ppermute | solution.py:111
  684.2 29.7 %collective-permute-start.3 = (bf16[16,128,2,128]{3,1,2,0:T(8,128)(2,1)S(1)}, bf16[16,128,2,128]{3,1,2,0:T(8,128)(2,1)S(1)}, u32[]{:S(2)}, u32[]{:S(2)}) collective-permute-start(bf16[16,128,2,128]{3,1,2,0:T(8,128)(2,1)S(1)} %get-tuple-element.440), channel_id=1, source_target_pairs={{0,8},{8,16},{16,24},{24,0},{1,9},{9,17},{17,25},{25,1},{2,10},{10... | collective-permute-start | bytes 3145736 | tf_op jit(solution)/shard_map/while/body/eval_jaxpr/ppermute | solution.py:111
  684.3 28.0 %collective-permute-start.5 = (s32[16,128]{1,0:T(8,128)S(1)}, s32[16,128]{1,0:T(8,128)S(1)}, u32[]{:S(2)}, u32[]{:S(2)}) collective-permute-start(s32[16,128]{1,0:T(8,128)S(1)} %get-tuple-element.442), channel_id=1, source_target_pairs={{0,8},{8,16},{16,24},{24,0},{1,9},{9,17},{17,25},{25,1},{2,10},{10... | collective-permute-start | bytes 24584 | tf_op jit(solution)/shard_map/while/body/eval_jaxpr/ppermute | solution.py:111
  684.3 50.5 %collective-permute-start.4 = (bf16[16,128,2,128]{3,1,2,0:T(8,128)(2,1)}, bf16[16,128,2,128]{3,1,2,0:T(8,128)(2,1)}, u32[]{:S(2)}, u32[]{:S(2)}) collective-permute-start(bf16[16,128,2,128]{3,1,2,0:T(8,128)(2,1)} %get-tuple-element.441), channel_id=1, source_target_pairs={{0,8},{8,16},{16,24},{24,0},{1,9},{9,17},{17,25},{25,1},{2,10},{10... | collective-permute-start | bytes 3145736 | tf_op jit(solution)/shard_map/while/body/eval_jaxpr/ppermute | solution.py:111
  684.9 94.8 %collective-permute-start.6 = (f32[16,2,128,128]{3,2,1,0:T(8,128)}, f32[16,2,128,128]{3,2,1,0:T(8,128)}, u32[]{:S(2)}, u32[]{:S(2)}) collective-permute-start(f32[16,2,128,128]{3,2,1,0:T(8,128)} %get-tuple-element.444), channel_id=1, source_target_pairs={{0,8},{8,16},{16,24},{24,0},{1,9},{9,17},{17,25},{25,1},{2,10},{10... | collective-permute-start | bytes 6291464 | tf_op jit(solution)/shard_map/while/body/eval_jaxpr/ppermute | solution.py:111
  689.2 124.8 %collective-permute-start.7 = (f32[16,2,128,128]{3,2,1,0:T(8,128)}, f32[16,2,128,128]{3,2,1,0:T(8,128)}, u32[]{:S(2)}, u32[]{:S(2)}) collective-permute-start(f32[16,2,128,128]{3,2,1,0:T(8,128)} %get-tuple-element.445), channel_id=1, source_target_pairs={{0,8},{8,16},{16,24},{24,0},{1,9},{9,17},{17,25},{25,1},{2,10},{10... | collective-permute-start | bytes 6291464 | tf_op jit(solution)/shard_map/while/body/eval_jaxpr/ppermute | solution.py:111
  766.7 47.3 %copy-start.16 = (pred[16,128,128]{2,1,0:T(8,128)(4,1)S(1)}, pred[16,128,128]{2,1,0:T(8,128)(4,1)}, u32[]{:S(2)}) copy-start(pred[16,128,128]{2,1,0:T(8,128)(4,1)} %broadcast_compare_fusion.6) | copy-start | bytes 786436 | tf_op jit(solution)/shard_map/while
  766.7 47.3 %copy-start.33 = (f32[16,2,128,8]{2,3,1,0:T(8,128)S(1)}, f32[16,2,128,8]{2,3,1,0:T(8,128)}, u32[]{:S(2)}) copy-start(f32[16,2,128,8]{2,3,1,0:T(8,128)} %copy-done.32) | copy-start | bytes 393220 | tf_op jit(solution)/shard_map/while
  790.0 38.3 %copy-start.9 = (bf16[16,128,2,128]{3,1,2,0:T(8,128)(2,1)S(1)}, bf16[16,128,2,128]{3,1,2,0:T(8,128)(2,1)}, u32[]{:S(2)}) copy-start(bf16[16,128,2,128]{3,1,2,0:T(8,128)(2,1)} %copy.200) | copy-start | bytes 3145732 | tf_op jit(solution)/shard_map/while
  790.0 38.3 %copy-start.31 = (f32[16,2,128,8]{2,3,1,0:T(8,128)S(1)}, f32[16,2,128,8]{2,3,1,0:T(8,128)}, u32[]{:S(2)}) copy-start(f32[16,2,128,8]{2,3,1,0:T(8,128)} %copy-done.30) | copy-start | bytes 393220 | tf_op jit(solution)/shard_map/while
  790.0 38.3 %copy-start.39 = (s32[16,128]{1,0:T(8,128)S(1)}, s32[16,128]{1,0:T(8,128)}, u32[]{:S(2)}) copy-start(s32[16,128]{1,0:T(8,128)} %copy.202) | copy-start | bytes 24580 | tf_op jit(solution)/shard_map/while
  828.4 29.7 %collective-permute-start.3 = (bf16[16,128,2,128]{3,1,2,0:T(8,128)(2,1)S(1)}, bf16[16,128,2,128]{3,1,2,0:T(8,128)(2,1)S(1)}, u32[]{:S(2)}, u32[]{:S(2)}) collective-permute-start(bf16[16,128,2,128]{3,1,2,0:T(8,128)(2,1)S(1)} %get-tuple-element.440), channel_id=1, source_target_pairs={{0,8},{8,16},{16,24},{24,0},{1,9},{9,17},{17,25},{25,1},{2,10},{10... | collective-permute-start | bytes 3145736 | tf_op jit(solution)/shard_map/while/body/eval_jaxpr/ppermute | solution.py:111
  828.4 28.0 %collective-permute-start.5 = (s32[16,128]{1,0:T(8,128)S(1)}, s32[16,128]{1,0:T(8,128)S(1)}, u32[]{:S(2)}, u32[]{:S(2)}) collective-permute-start(s32[16,128]{1,0:T(8,128)S(1)} %get-tuple-element.442), channel_id=1, source_target_pairs={{0,8},{8,16},{16,24},{24,0},{1,9},{9,17},{17,25},{25,1},{2,10},{10... | collective-permute-start | bytes 24584 | tf_op jit(solution)/shard_map/while/body/eval_jaxpr/ppermute | solution.py:111
  828.5 50.5 %collective-permute-start.4 = (bf16[16,128,2,128]{3,1,2,0:T(8,128)(2,1)}, bf16[16,128,2,128]{3,1,2,0:T(8,128)(2,1)}, u32[]{:S(2)}, u32[]{:S(2)}) collective-permute-start(bf16[16,128,2,128]{3,1,2,0:T(8,128)(2,1)} %get-tuple-element.441), channel_id=1, source_target_pairs={{0,8},{8,16},{16,24},{24,0},{1,9},{9,17},{17,25},{25,1},{2,10},{10... | collective-permute-start | bytes 3145736 | tf_op jit(solution)/shard_map/while/body/eval_jaxpr/ppermute | solution.py:111
  829.1 94.8 %collective-permute-start.6 = (f32[16,2,128,128]{3,2,1,0:T(8,128)}, f32[16,2,128,128]{3,2,1,0:T(8,128)}, u32[]{:S(2)}, u32[]{:S(2)}) collective-permute-start(f32[16,2,128,128]{3,2,1,0:T(8,128)} %get-tuple-element.444), channel_id=1, source_target_pairs={{0,8},{8,16},{16,24},{24,0},{1,9},{9,17},{17,25},{25,1},{2,10},{10... | collective-permute-start | bytes 6291464 | tf_op jit(solution)/shard_map/while/body/eval_jaxpr/ppermute | solution.py:111
  833.4 123.9 %collective-permute-start.7 = (f32[16,2,128,128]{3,2,1,0:T(8,128)}, f32[16,2,128,128]{3,2,1,0:T(8,128)}, u32[]{:S(2)}, u32[]{:S(2)}) collective-permute-start(f32[16,2,128,128]{3,2,1,0:T(8,128)} %get-tuple-element.445), channel_id=1, source_target_pairs={{0,8},{8,16},{16,24},{24,0},{1,9},{9,17},{17,25},{25,1},{2,10},{10... | collective-permute-start | bytes 6291464 | tf_op jit(solution)/shard_map/while/body/eval_jaxpr/ppermute | solution.py:111
  910.9 46.4 %copy-start.16 = (pred[16,128,128]{2,1,0:T(8,128)(4,1)S(1)}, pred[16,128,128]{2,1,0:T(8,128)(4,1)}, u32[]{:S(2)}) copy-start(pred[16,128,128]{2,1,0:T(8,128)(4,1)} %broadcast_compare_fusion.6) | copy-start | bytes 786436 | tf_op jit(solution)/shard_map/while
  910.9 46.4 %copy-start.33 = (f32[16,2,128,8]{2,3,1,0:T(8,128)S(1)}, f32[16,2,128,8]{2,3,1,0:T(8,128)}, u32[]{:S(2)}) copy-start(f32[16,2,128,8]{2,3,1,0:T(8,128)} %copy-done.32) | copy-start | bytes 393220 | tf_op jit(solution)/shard_map/while
  971.7 29.7 %collective-permute-start.3 = (bf16[16,128,2,128]{3,1,2,0:T(8,128)(2,1)S(1)}, bf16[16,128,2,128]{3,1,2,0:T(8,128)(2,1)S(1)}, u32[]{:S(2)}, u32[]{:S(2)}) collective-permute-start(bf16[16,128,2,128]{3,1,2,0:T(8,128)(2,1)S(1)} %get-tuple-element.440), channel_id=1, source_target_pairs={{0,8},{8,16},{16,24},{24,0},{1,9},{9,17},{17,25},{25,1},{2,10},{10... | collective-permute-start | bytes 3145736 | tf_op jit(solution)/shard_map/while/body/eval_jaxpr/ppermute | solution.py:111
  971.7 28.0 %collective-permute-start.5 = (s32[16,128]{1,0:T(8,128)S(1)}, s32[16,128]{1,0:T(8,128)S(1)}, u32[]{:S(2)}, u32[]{:S(2)}) collective-permute-start(s32[16,128]{1,0:T(8,128)S(1)} %get-tuple-element.442), channel_id=1, source_target_pairs={{0,8},{8,16},{16,24},{24,0},{1,9},{9,17},{17,25},{25,1},{2,10},{10... | collective-permute-start | bytes 24584 | tf_op jit(solution)/shard_map/while/body/eval_jaxpr/ppermute | solution.py:111
  971.8 50.5 %collective-permute-start.4 = (bf16[16,128,2,128]{3,1,2,0:T(8,128)(2,1)}, bf16[16,128,2,128]{3,1,2,0:T(8,128)(2,1)}, u32[]{:S(2)}, u32[]{:S(2)}) collective-permute-start(bf16[16,128,2,128]{3,1,2,0:T(8,128)(2,1)} %get-tuple-element.441), channel_id=1, source_target_pairs={{0,8},{8,16},{16,24},{24,0},{1,9},{9,17},{17,25},{25,1},{2,10},{10... | collective-permute-start | bytes 3145736 | tf_op jit(solution)/shard_map/while/body/eval_jaxpr/ppermute | solution.py:111
  972.4 94.8 %collective-permute-start.6 = (f32[16,2,128,128]{3,2,1,0:T(8,128)}, f32[16,2,128,128]{3,2,1,0:T(8,128)}, u32[]{:S(2)}, u32[]{:S(2)}) collective-permute-start(f32[16,2,128,128]{3,2,1,0:T(8,128)} %get-tuple-element.444), channel_id=1, source_target_pairs={{0,8},{8,16},{16,24},{24,0},{1,9},{9,17},{17,25},{25,1},{2,10},{10... | collective-permute-start | bytes 6291464 | tf_op jit(solution)/shard_map/while/body/eval_jaxpr/ppermute | solution.py:111
  976.7 123.1 %collective-permute-start.7 = (f32[16,2,128,128]{3,2,1,0:T(8,128)}, f32[16,2,128,128]{3,2,1,0:T(8,128)}, u32[]{:S(2)}, u32[]{:S(2)}) collective-permute-start(f32[16,2,128,128]{3,2,1,0:T(8,128)} %get-tuple-element.445), channel_id=1, source_target_pairs={{0,8},{8,16},{16,24},{24,0},{1,9},{9,17},{17,25},{25,1},{2,10},{10... | collective-permute-start | bytes 6291464 | tf_op jit(solution)/shard_map/while/body/eval_jaxpr/ppermute | solution.py:111
  1054.2 45.6 %copy-start.16 = (pred[16,128,128]{2,1,0:T(8,128)(4,1)S(1)}, pred[16,128,128]{2,1,0:T(8,128)(4,1)}, u32[]{:S(2)}) copy-start(pred[16,128,128]{2,1,0:T(8,128)(4,1)} %broadcast_compare_fusion.6) | copy-start | bytes 786436 | tf_op jit(solution)/shard_map/while
  1054.2 45.6 %copy-start.33 = (f32[16,2,128,8]{2,3,1,0:T(8,128)S(1)}, f32[16,2,128,8]{2,3,1,0:T(8,128)}, u32[]{:S(2)}) copy-start(f32[16,2,128,8]{2,3,1,0:T(8,128)} %copy-done.32) | copy-start | bytes 393220 | tf_op jit(solution)/shard_map/while
  1114.1 122.3 %collective-permute-start.8 = (f32[16,2,128,128]{3,2,1,0:T(8,128)}, f32[16,2,128,128]{3,2,1,0:T(8,128)}, u32[]{:S(2)}, u32[]{:S(2)}) collective-permute-start(f32[16,2,128,128]{3,2,1,0:T(8,128)} %get-tuple-element.124), channel_id=1, source_target_pairs={{0,8},{8,16},{16,24},{24,0},{1,9},{9,17},{17,25},{25,1},{2,10},{10... | collective-permute-start | bytes 6291464 | tf_op jit(solution)/shard_map/ppermute | solution.py:111
  1132.1 41.7 %collective-permute-start.9 = (bf16[16,2,128,128]{3,2,1,0:T(8,128)(2,1)S(1)}, bf16[16,2,128,128]{3,2,1,0:T(8,128)(2,1)S(1)}, u32[]{:S(2)}, u32[]{:S(2)}) collective-permute-start(bf16[16,2,128,128]{3,2,1,0:T(8,128)(2,1)S(1)} %convert.34), channel_id=1, source_target_pairs={{0,8},{8,16},{16,24},{24,0},{1,9},{9,17},{17,25},{25,1},{2,10},{10... | collective-permute-start | bytes 3145736 | tf_op jit(solution)/shard_map/ppermute | solution.py:111
  1182.1 284.0 %reduce-scatter.7.cloned.1.call-start = ((), (), s32[]{:S(2)}) async-start(), calls=%async_computation.9 | async-start | bytes 2162688 | tf_op jit(solution)/shard_map/reduce_scatter | solution.py:117
  1247.9 571.7 %reduce-scatter.5.cloned.1.call-start = ((), (), s32[]{:S(2)}) async-start(), calls=%async_computation.8 | async-start | bytes 17301504 | tf_op jit(solution)/shard_map/reduce_scatter | solution.py:117
  1282.0 902.5 %reduce-scatter.11.cloned.1.call-start = ((), (), s32[]{:S(2)}) async-start(), calls=%async_computation.11 | async-start | bytes 17301504 | tf_op jit(solution)/shard_map/reduce_scatter | solution.py:117
  (48 other events, 847.4 us)
Sparse Core Ops, SparseCore 0:
  11.0 56.5 all-gather.4
  70.5 52.8 all-gather.6
  126.4 76.0 all-gather.8
  205.3 75.6 all-gather.10
  1182.2 135.9 reduce-scatter.8
  1320.9 137.5 reduce-scatter.6
  1461.4 358.2 reduce-scatter.4
  1822.5 361.9 reduce-scatter.10
where the time goes:
time: 2200 us; the launch traced here: 2190 us
  waiting for transfers between devices  1150 us (52%)
  matrix products  529 us (24%)
  local copies, waits for them, and re-layouts  223 us (10%)
  other arithmetic  171 us (8%)
  blocking collectives  79.3 us (4%)
  starting transfers between devices  22.5 us (1%)
    reduce_scatter x4, waiting for transfers between devices, sum_to_shards(): return lax.psum_scatter(part_sum, ALL_AXES, scatter_dimension=0, tiled=True)  718 us
    ppermute x26, waiting for transfers between devices, pass_on(): return lax.ppermute(local_part, 'cp', shift_perm)  333 us
    all_gather x4, waiting for transfers between devices, collect_full(): return lax.all_gather(local_part, ALL_AXES, axis=0, tiled=True)  95.6 us
    unnamed x2, blocking collectives  79.3 us
    unnamed x71, local copies, waits for them, and re-layouts  74.8 us
    dot_general x4, matrix products, attn_fwd_block(): jnp.einsum('bkigj,bjkd->bkigd', att_probs.astype(jnp.bfloat16), v_blk, pr...  68 us
    dot_general x4, matrix products, attn_bwd_block(): jnp.einsum('bkigj,bjkd->bkigd', grad_scores, k_blk, preferred_element_typ...  60.4 us
    dot_general x4, matrix products, attn_bwd_block(): jnp.einsum('bkigj,bikgd->bkjd', att_probs.astype(jnp.bfloat16), gout_grp,...  55.7 us
  transfers between devices with their start and end apart: 34, of which 20 were waited for; matrix products, arithmetic and copies ran while one was open for 30% of the time, Pallas kernels for 0%

commit v1 on v0

v1 whole, which is shorter than its diff:
```python
import functools

import jax
import jax.numpy as jnp
from jax import lax
from jax.experimental import pallas as pl
from jax.experimental.pallas import tpu as pltpu
from jax.sharding import PartitionSpec as P


HEAD_DIM = 128
HALF = HEAD_DIM // 2
ROPE_THETA = 1000000.0
RMS_EPS = 1e-5
NEG_BIG = -1e30
SCALE = HEAD_DIM ** -0.5
LOG2E = 1.4426950408889634
ALL_AXES = ('fsdp', 'cp')
F32 = jnp.float32
BF16 = jnp.bfloat16
VMEM_LIMIT = 60 * 1024 * 1024


def dot_nn(a, b):
    return lax.dot_general(a, b, (((1,), (0,)), ((), ())), preferred_element_type=F32)


def dot_nt(a, b):
    return lax.dot_general(a, b, (((1,), (1,)), ((), ())), preferred_element_type=F32)


def dot_tn(a, b):
    return lax.dot_general(a, b, (((0,), (0,)), ((), ())), preferred_element_type=F32)


def params():
    return pltpu.CompilerParams(vmem_limit_bytes=VMEM_LIMIT, dimension_semantics=('arbitrary',))


def cost(flops, nbytes):
    return pl.CostEstimate(flops=int(flops), bytes_accessed=int(nbytes), transcendentals=0)


def whole(shape, index=None):
    index = index or (0,) * len(shape)
    return pl.BlockSpec(shape, lambda i: index, pipeline_mode=pl.Buffered(1))


def norm_kv_body(kv_heads, x_ref, gain_ref, wkv_ref, cos_ref, sin_ref, r_ref, *kv_refs):
    x = x_ref[...].astype(F32)
    inv = lax.rsqrt(jnp.mean(x * x, axis=-1, keepdims=True) + RMS_EPS)
    r = (x * inv * gain_ref[...]).astype(BF16)
    r_ref[...] = r
    kv = dot_nn(r, wkv_ref[...])
    cos, sin = cos_ref[...], sin_ref[...]
    for h in range(kv_heads):
        k0 = 2 * h * HEAD_DIM
        a = kv[:, k0:k0 + HEAD_DIM]
        kv_refs[h][...] = (a * cos + pltpu.roll(a, HALF, 1) * sin).astype(BF16)
        kv_refs[kv_heads + h][...] = kv[:, k0 + HEAD_DIM:k0 + 2 * HEAD_DIM].astype(BF16)


def norm_kv(x, gain_row, wkv, cos_rows, sin_rows, kv_heads):
    tokens, width = x.shape
    bm = min(256, tokens)
    rows = lambda w: pl.BlockSpec((bm, w), lambda i: (i, 0))
    head = jax.ShapeDtypeStruct((tokens, HEAD_DIM), BF16)
    return pl.pallas_call(
        functools.partial(norm_kv_body, kv_heads),
        grid=(tokens // bm,),
        in_specs=[rows(width), whole((1, width)), whole(wkv.shape), rows(HEAD_DIM), rows(HEAD_DIM)],
        out_specs=[rows(width)] + [rows(HEAD_DIM)] * (2 * kv_heads),
        out_shape=[jax.ShapeDtypeStruct((tokens, width), BF16)] + [head] * (2 * kv_heads),
        compiler_params=params(),
        cost_estimate=cost(2 * tokens * width * wkv.shape[1] * 2, 4 * tokens * width),
        name='norm_kv',
    )(x, gain_row, wkv, cos_rows, sin_rows)


def q_do_body(heads, r_ref, dy_ref, wq_ref, wo_ref, cos_ref, sin_ref, q_ref, do_ref):
    lin = dot_nn(r_ref[...], wq_ref[...])
    cos, sin = cos_ref[...], sin_ref[...]
    for h in range(heads):
        lanes = slice(h * HEAD_DIM, (h + 1) * HEAD_DIM)
        a = lin[:, lanes]
        q_ref[:, lanes] = (a * cos + pltpu.roll(a, HALF, 1) * sin).astype(BF16)
    do_ref[...] = dot_nt(dy_ref[...], wo_ref[...]).astype(BF16)


def q_do(r, dy, wqo, cos_rows, sin_rows, group, cols):
    tokens, width = r.shape
    bm = min(512, tokens)
    rows = lambda w: pl.BlockSpec((bm, w), lambda i: (i, 0))
    out = jax.ShapeDtypeStruct((tokens, cols), BF16)
    return pl.pallas_call(
        functools.partial(q_do_body, cols // HEAD_DIM),
        grid=(tokens // bm,),
        in_specs=[rows(width), rows(width), whole((width, cols), (0, group)), whole((cols, width), (group, 1)),
                  rows(HEAD_DIM), rows(HEAD_DIM)],
        out_specs=[rows(cols), rows(cols)],
        out_shape=[out, out],
        compiler_params=params(),
        cost_estimate=cost(4 * tokens * width * cols, 8 * tokens * width),
        name='q_do',
    )(r, dy, wqo, wqo, cos_rows, sin_rows)


def attn_body(n_blk, heads, per, q_ref, do_ref, *refs):
    k_refs, v_refs = refs[:n_blk], refs[n_blk:2 * n_blk]
    bias_ref, cos_ref, sin_ref = refs[2 * n_blk:2 * n_blk + 3]
    outs = refs[len(refs) - 2 - 2 * n_blk:]
    o_ref, dq_ref = outs[0], outs[1]
    dk_refs, dv_refs = outs[2:2 + n_blk], outs[2 + n_blk:]
    kc = jnp.concatenate([k[...] for k in k_refs], axis=0)
    vc = jnp.concatenate([v[...] for v in v_refs], axis=0)
    kt, vt = kc.T, vc.T
    bias = jnp.concatenate([bias_ref[0]] * per, axis=1)
    cos = jnp.concatenate([cos_ref[0]] * per, axis=1)
    sin = jnp.concatenate([sin_ref[0]] * per, axis=1)
    q_all, do_all, p_all, ds_all = [], [], [], []
    for c in range(heads // per):
        lanes = [slice((c * per + h) * HEAD_DIM, (c * per + h + 1) * HEAD_DIM) for h in range(per)]
        q = jnp.concatenate([q_ref[:, s] for s in lanes], axis=0)
        do = jnp.concatenate([do_ref[:, s] for s in lanes], axis=0)
        t = dot_nt(kc, q) * (SCALE * LOG2E) + bias
        e = jnp.exp2(t - jnp.max(t, axis=0, keepdims=True))
        inv_l = 1.0 / jnp.sum(e, axis=0, keepdims=True)
        o_t = (dot_nn(vt, e.astype(BF16)) * inv_l).astype(BF16)
        delta = jnp.sum(do.T.astype(F32) * o_t.astype(F32), axis=0, keepdims=True)
        p = e * inv_l
        ds = (p * (dot_nt(vc, do) - delta)).astype(BF16)
        dq_t = dot_nn(kt, ds) * SCALE
        a, b = dq_t[:HALF], dq_t[HALF:]
        dq_t = jnp.concatenate([a * cos + b * sin, b * cos - a * sin], axis=0).astype(BF16)
        o, dq = o_t.T, dq_t.T
        n_rows = o.shape[0] // per
        for h, s in enumerate(lanes):
            o_ref[:, s] = o[h * n_rows:(h + 1) * n_rows]
            dq_ref[:, s] = dq[h * n_rows:(h + 1) * n_rows]
        q_all.append(q)
        do_all.append(do)
        p_all.append(p.astype(BF16))
        ds_all.append(ds)
    dv = dot_nn(jnp.concatenate(p_all, axis=1), jnp.concatenate(do_all, axis=0))
    dk = dot_nn(jnp.concatenate(ds_all, axis=1), jnp.concatenate(q_all, axis=0))
    n_keys = kc.shape[0] // n_blk
    for b in range(n_blk):
        dk_refs[b][...] = dk[b * n_keys:(b + 1) * n_keys]
        dv_refs[b][...] = dv[b * n_keys:(b + 1) * n_keys]


def attention(q, do, ks, vs, bias, cos_t, sin_t, o_prev, group, n_seq, width):
    tokens, cols = q.shape
    rows = tokens // n_seq
    n_blk, heads = len(ks), cols // HEAD_DIM
    per = 2
    blk = pl.BlockSpec((rows, cols), lambda i: (i, 0))
    kv = pl.BlockSpec((rows, HEAD_DIM), lambda i: (i, 0))
    table = pl.BlockSpec((1, HALF, rows), lambda i: (i, 0, 0))
    in_specs = [blk, blk] + [kv] * (2 * n_blk) + [pl.BlockSpec((1, n_blk * rows, rows), lambda i: (i, 0, 0)), table, table]
    args = [q, do, *ks, *vs, bias, cos_t, sin_t]
    aliases = {}
    if o_prev is not None:
        aliases[len(args)] = 0
        in_specs.append(pl.BlockSpec(memory_space=pl.ANY))
        args.append(o_prev)
    part = jax.ShapeDtypeStruct((tokens, HEAD_DIM), F32)
    return pl.pallas_call(
        functools.partial(attn_body, n_blk, heads, per),
        grid=(n_seq,),
        in_specs=in_specs,
        out_specs=[pl.BlockSpec((rows, cols), lambda i: (i, group)), blk] + [kv] * (2 * n_blk),
        out_shape=[jax.ShapeDtypeStruct((tokens, width), BF16), jax.ShapeDtypeStruct((tokens, cols), BF16)]
        + [part] * (2 * n_blk),
        input_output_aliases=aliases,
        compiler_params=params(),
        cost_estimate=cost(24 * tokens * cols * n_blk * rows, 10 * tokens * cols),
        name='attention',
    )(*args)


def out_proj_body(x_ref, o_ref, wo_ref, res_ref):
    res_ref[...] = (x_ref[...].astype(F32) + dot_nn(o_ref[...], wo_ref[...])).astype(BF16)


def out_proj(x, o, wqo):
    tokens, width = x.shape
    bm = min(512, tokens)
    rows = pl.BlockSpec((bm, width), lambda i: (i, 0))
    return pl.pallas_call(
        out_proj_body,
        grid=(tokens // bm,),
        in_specs=[rows, rows, whole((o.shape[1], width), (0, 1))],
        out_specs=rows,
        out_shape=jax.ShapeDtypeStruct((tokens, width), BF16),
        compiler_params=params(),
        cost_estimate=cost(2 * tokens * width * o.shape[1], 8 * tokens * width),
        name='out_proj',
    )(x, o, wqo)


def dr_query_body(n, *refs):
    wq = refs[n][...]
    total = None
    for g in range(n):
        cols = refs[g].shape[1]
        part = dot_nt(refs[g][...], wq[:, g * cols:(g + 1) * cols])
        total = part if total is None else total + part
    refs[n + 1][...] = total


def dr_query(dqs, wqo):
    tokens, cols = dqs[0].shape
    width = wqo.shape[0]
    bm = min(256, tokens)
    rows = lambda w: pl.BlockSpec((bm, w), lambda i: (i, 0))
    return pl.pallas_call(
        functools.partial(dr_query_body, len(dqs)),
        grid=(tokens // bm,),
        in_specs=[rows(cols)] * len(dqs) + [whole((width, cols * len(dqs)))],
        out_specs=rows(width),
        out_shape=jax.ShapeDtypeStruct((tokens, width), F32),
        compiler_params=params(),
        cost_estimate=cost(2 * tokens * width * cols * len(dqs), 8 * tokens * width),
        name='dr_query',
    )(*dqs, wqo)


def norm_back_body(x_ref, dy_ref, dr_ref, dkv0_ref, dkv1_ref, wkv_ref, gain_ref, gh_ref, gg_ref):
    x = x_ref[...].astype(F32)
    inv = lax.rsqrt(jnp.mean(x * x, axis=-1, keepdims=True) + RMS_EPS)
    n = x * inv
    dr = dr_ref[...] + dot_nt(jnp.concatenate([dkv0_ref[...], dkv1_ref[...]], axis=1), wkv_ref[...])
    prod = dr * n
    part = jnp.sum(prod.reshape(prod.shape[0] // 8, 8, prod.shape[1]), axis=0)

    @pl.when(pl.program_id(0) == 0)
    def _():
        gg_ref[...] = part

    @pl.when(pl.program_id(0) > 0)
    def _():
        gg_ref[...] = gg_ref[...] + part

    gain = gain_ref[...]
    mean = jnp.mean(prod * gain, axis=-1, keepdims=True)
    gh_ref[...] = (dy_ref[...].astype(F32) + inv * (dr * gain - n * mean)).astype(BF16)


def norm_back(x, dy, dr, dkvs, wkv, gain_row):
    tokens, width = x.shape
    bm = min(256, tokens)
    rows = lambda w: pl.BlockSpec((bm, w), lambda i: (i, 0))
    return pl.pallas_call(
        norm_back_body,
        grid=(tokens // bm,),
        in_specs=[rows(width)] * 3 + [rows(2 * HEAD_DIM)] * 2 + [whole(wkv.shape), whole((1, width))],
        out_specs=[rows(width), pl.BlockSpec((8, width), lambda i: (0, 0))],
        out_shape=[jax.ShapeDtypeStruct((tokens, width), BF16), jax.ShapeDtypeStruct((8, width), F32)],
        compiler_params=params(),
        cost_estimate=cost(4 * tokens * width * wkv.shape[1], 14 * tokens * width),
        name='norm_back',
    )(x, dy, dr, *dkvs, wkv, gain_row)


def solution(mesh):
    cp_size, fsdp_size = mesh.shape['cp'], mesh.shape['fsdp']

    def shift(values, step):
        return lax.ppermute(values, 'cp', [(i, (i + step) % cp_size) for i in range(cp_size)])

    def swap(values, axis, bit):
        return lax.ppermute(values, axis, [(i, i ^ bit) for i in range(mesh.shape[axis])])

    def bit_set(axis, bit):
        return (lax.axis_index(axis) & bit) != 0

    def after(values, gate):
        return lax.optimization_barrier((tuple(values), tuple(gate)))[0]

    def gather_small(shard):
        def join(own, axis, bit, at):
            other = swap(own, axis, bit)
            upper = bit_set(axis, bit)
            return jnp.stack([jnp.where(upper, other, own), jnp.where(upper, own, other)], axis=at)

        full = join(shard, 'cp', 1, 0)
        full = join(full, 'cp', 2, 0)
        full = full.reshape((cp_size,) + shard.shape)
        full = join(full, 'fsdp', 4, 0)
        full = join(full, 'fsdp', 2, 1)
        full = join(full, 'fsdp', 1, 2)
        return full.reshape((fsdp_size * cp_size * shard.shape[0],) + shard.shape[1:])

    def scatter_small(total):
        part = total
        for axis, bits in (('fsdp', (4, 2, 1)), ('cp', (2, 1))):
            for bit in bits:
                half = part.shape[0] // 2
                upper = bit_set(axis, bit)
                low, high = part[:half], part[half:]
                part = jnp.where(upper, high, low) + swap(jnp.where(upper, low, high), axis, bit)
        return part

    def scatter_fsdp(part_sum):
        return lax.psum_scatter(part_sum, 'fsdp', scatter_dimension=0, tiled=True)

    def scatter_cp(part_sum):
        return lax.psum_scatter(part_sum, 'cp', scatter_dimension=0, tiled=True)

    def block(hidden, tok_pos, grad_out, norm_gain, w_query, w_key, w_value, w_out):
        n_seq, n_rows, width = hidden.shape
        tokens = n_seq * n_rows
        q_cols, kv_cols = w_query.shape[1], w_key.shape[1]
        kv_heads = kv_cols // HEAD_DIM
        cols = q_cols // kv_heads
        x = hidden.reshape(tokens, width)
        dy = grad_out.reshape(tokens, width)

        wqo = lax.all_gather(jnp.concatenate([w_query, w_out], axis=1), ALL_AXES, axis=0, tiled=True)
        gain_row = gather_small(norm_gain).reshape(1, width)
        wkv = gather_small(jnp.concatenate([w_key[:, :HEAD_DIM], w_value[:, :HEAD_DIM], w_key[:, HEAD_DIM:], w_value[:, HEAD_DIM:]], axis=1))

        inv_freq = ROPE_THETA ** (-jnp.arange(HALF, dtype=F32) / HALF)
        pos_f = tok_pos.astype(F32)
        angles = pos_f.reshape(tokens, 1) * inv_freq
        cos, sin = jnp.cos(angles), jnp.sin(angles)
        cos_rows = jnp.concatenate([cos, cos], axis=1)
        sin_rows = jnp.concatenate([-sin, sin], axis=1)
        angles_t = pos_f[:, None, :] * inv_freq[None, :, None]
        cos_t, sin_t = jnp.cos(angles_t), jnp.sin(angles_t)
        key_pos = jnp.concatenate([tok_pos] + [shift(tok_pos, d) for d in range(1, cp_size)], axis=1)
        bias = jnp.where(key_pos[:, :, None] <= tok_pos[:, None, :], 0.0, NEG_BIG).astype(F32)

        r, *kv = norm_kv(x, gain_row, wkv, cos_rows, sin_rows, kv_heads)

        keys, values, gate = [], [], ()
        for g in range(kv_heads):
            k, v = after((kv[g], kv[kv_heads + g]), gate)
            ks, vs = [k], [v]
            for _ in range(cp_size - 1):
                gate = (ks[-1], vs[-1])
                ks.append(shift(ks[-1], 1))
                vs.append(shift(vs[-1], -1))
            keys.append(ks)
            values.append([vs[0]] + vs[:0:-1])

        def ring_step(s, sums, parts, gate):
            moved = shift(sums[0], 1), shift(sums[1], -1)
            dk, dv = after(moved, gate)
            b = s + 1
            return dk + parts[b % cp_size], dv + parts[cp_size + (cp_size - b) % cp_size]

        def attend(g, o):
            q, do = q_do(r, dy, wqo, cos_rows, sin_rows, g, cols)
            o, dq, *parts = attention(q, do, keys[g], values[g], bias, cos_t, sin_t, o, g, n_seq, q_cols)
            return o, dq, parts, (parts[1], parts[2 * cp_size - 1])

        o, dq0, parts0, sums0 = attend(0, None)
        o, dq1, parts1, sums1 = attend(1, o)
        sums0 = ring_step(1, sums0, parts0, (dq1,))
        part_wo = dot_tn(o, dy)
        half_wo = scatter_fsdp(part_wo)
        part_wq0 = dot_tn(r, dq0)
        half_wq0 = scatter_fsdp(part_wq0)
        part_wq1 = dot_tn(r, dq1)
        half_wq1 = scatter_fsdp(part_wq1)
        sums0 = ring_step(2, sums0, parts0, (part_wo, part_wq0, part_wq1))
        sums1 = ring_step(1, sums1, parts1, (part_wo, part_wq0, part_wq1))
        dr = dr_query((dq0, dq1), wqo)
        result = out_proj(x, o, wqo)
        sums0 = ring_step(3, sums0, parts0, (dr,))
        sums1 = ring_step(2, sums1, parts1, (dr, result))

        def pair_back(sums):
            a = sums[0] * SCALE
            dk = a * cos_rows - jnp.concatenate([a[:, HALF:], a[:, :HALF]], axis=1) * sin_rows
            return jnp.concatenate([dk, sums[1]], axis=1).astype(BF16)

        dkv0 = pair_back(sums0)
        part_wkv0 = dot_tn(r, dkv0)
        half_wkv0 = scatter_fsdp(after((part_wkv0,), (half_wq0, half_wq1))[0])
        grad_wo, grad_wq0, grad_wq1 = scatter_cp(half_wo), scatter_cp(half_wq0), scatter_cp(half_wq1)
        sums1 = ring_step(3, sums1, parts1, (part_wkv0,))
        dkv1 = pair_back(sums1)
        part_wkv1 = dot_tn(r, dkv1)
        half_wkv1 = scatter_fsdp(after((part_wkv1,), (grad_wo, grad_wq0, grad_wq1, half_wkv0))[0])
        grad_wkv0, grad_wkv1 = scatter_cp(half_wkv0), scatter_cp(half_wkv1)
        grad_hidden, gain_parts = norm_back(x, dy, dr, (dkv0, dkv1), wkv, gain_row)
        grad_gain = scatter_small(jnp.sum(gain_parts, axis=0))
        grad_wk = jnp.concatenate([grad_wkv0[:, :HEAD_DIM], grad_wkv1[:, :HEAD_DIM]], axis=1)
        grad_wv = jnp.concatenate([grad_wkv0[:, HEAD_DIM:], grad_wkv1[:, HEAD_DIM:]], axis=1)
        grad_wq = jnp.concatenate([grad_wq0, grad_wq1], axis=1)
        return (result.reshape(hidden.shape), grad_hidden.reshape(hidden.shape), grad_wq, grad_wk, grad_wv,
                grad_wo, grad_gain)

    row_spec = P('fsdp', 'cp', None)
    pos_spec = P('fsdp', 'cp')
    weight_spec = P(ALL_AXES, None)
    gain_spec = P(ALL_AXES)
    return jax.shard_map(block, mesh=mesh, in_specs=(row_spec, pos_spec, row_spec, gain_spec, weight_spec, weight_spec, weight_spec, weight_spec), out_specs=(row_spec, row_spec, weight_spec, weight_spec, weight_spec, weight_spec, gain_spec), check_vma=False)
```

time: 2200 us -> 959 us (0.44)
  waiting for transfers between devices: 1150 us -> 490 us
  matrix products: 529 us -> 66.2 us
  Pallas kernels: 0 us -> 250 us
  local copies, waits for them, and re-layouts: 223 us -> 7.47 us
  other arithmetic: 171 us -> 34.4 us
  blocking collectives: 79.3 us -> 0 us
  starting transfers between devices: 22.5 us -> 89 us
    reduce_scatter x4 -> x10, waiting for transfers between devices: 718 us -> 137 us  [the longest x5 87 us: scatter_cp(): return lax.psum_scatter(part_sum, 'cp', scatter_dimension=0, tiled=True)]
    dot_general x39 -> x5, matrix products: 529 us -> 66.2 us  [dot_tn(): lax.dot_general(a, b, (((0,), (0,)), ((), ())), preferred_element_type=F32)]
    pallas_call x0 -> x8, Pallas kernels: none -> 250 us  [the longest x2 115 us: attention(): pl.pallas_call(functools.partial(attn_body, n_blk, heads, per), grid=(n_s...]
    all_gather x4 -> x1, waiting for transfers between devices: 95.6 us -> 0.02 us  [block(): lax.all_gather(jnp.concatenate([w_query, w_out], axis=1), ALL_AXES, axis=...]
    unnamed x2 -> x0, blocking collectives: 79.3 us -> none
    unnamed x71 -> x54, local copies, waits for them, and re-layouts: 74.8 us -> 3.78 us
    ppermute x26 -> x42, starting transfers between devices: 22.2 us -> 88.5 us  [the longest x27 69.7 us: shift(): lax.ppermute(values, 'cp', [(i, (i + step) % cp_size) for i in range(cp_s...]
    while x90 -> x0, local copies, waits for them, and re-layouts: 57.7 us -> none  [the longest x2 20.1 us: shard_fn(): lax.fori_loop(1, cp_size, fwd_step, (k_rot, v_val, tok_pos, own_stats))[3]]
  transfers between devices with their start and end apart: 34 -> 53, of which waited for: 20 -> 33; matrix products, arithmetic and copies ran while one was open for 30% -> 9% of each run, Pallas kernels for 0% -> 20%
where the time goes in v1:
time: 959 us; the launch traced here: 951 us
  waiting for transfers between devices  490 us (51%)
  Pallas kernels  250 us (26%)
  starting transfers between devices  89 us (9%)
  matrix products  66.2 us (7%)
  other arithmetic  34.4 us (4%)
  between operations  14.6 us (2%)
    ppermute x27, waiting for transfers between devices, shift(): lax.ppermute(values, 'cp', [(i, (i + step) % cp_size) for i in range(cp_s...  324 us
    pallas_call x2, Pallas kernels, attention(): pl.pallas_call(functools.partial(attn_body, n_blk, heads, per), grid=(n_s...  115 us
    reduce_scatter x5, waiting for transfers between devices, scatter_cp(): return lax.psum_scatter(part_sum, 'cp', scatter_dimension=0, tiled=True)  87 us
    ppermute x27, starting transfers between devices, shift(): lax.ppermute(values, 'cp', [(i, (i + step) % cp_size) for i in range(cp_s...  69.7 us
    dot_general x5, matrix products, dot_tn(): lax.dot_general(a, b, (((0,), (0,)), ((), ())), preferred_element_type=F32)  66.2 us
    reduce_scatter x5, waiting for transfers between devices, scatter_fsdp(): return lax.psum_scatter(part_sum, 'fsdp', scatter_dimension=0, tiled=True)  50 us
    pallas_call x2, Pallas kernels, q_do(): pl.pallas_call(functools.partial(q_do_body, cols // HEAD_DIM), grid=(toke...  49.2 us
    ppermute x15, waiting for transfers between devices, swap(): lax.ppermute(values, axis, [(i, i ^ bit) for i in range(mesh.shape[axis])])  29.3 us
  transfers between devices with their start and end apart: 53, of which 33 were waited for; matrix products, arithmetic and copies ran while one was open for 9% of the time, Pallas kernels for 20%

profile of v1, /device:TPU:0, one launch (start us, length us, event | category | flops | bytes accessed | tf_op | source)
XLA Modules:
  0.0 951.2 jit_solution(9998871401598917685)
XLA Ops:
  20.1 3.5 collective-permute-done.6
  26.0 7.2 collective-permute-done.7
  39.1 5.9 collective-permute-done.8
  45.3 3.7 fusion.4
  54.3 13.6 %norm_kv.1 = (bf16[2048,2048]{1,0:T(8,128)(2,1)}, bf16[2048,128]{1,0:T(8,128)(2,1)}, bf16[2048,128]{1,0:T(8,128)(2,1)}, bf16[2048,128]{1,0:T(8,128)(2,1)}, bf16[2048,128]{1,0:T(8,128)(2,1)}) custom-call(bf16[2048,2048]{1,0:T(8,128)(2,1)} %bitcast.67, f32[1,2048]{1,0:T(1,128)} %reshape_reshape.3.gain_ref, bf16[2048,512]{1,0:T(8,128)(2,1)} %bitcast.74, ...), custom_call_target="tpu_custom_call" | custom-call | flops 8589934592 | bytes 16777216 | tf_op jit(solution)/shard_map/norm_kv/pallas_call | solution.py:68
  70.7 6.1 collective-permute-start.12
  76.8 19.9 %collective-permute-done.10.refs_1_ = bf16[2048,128]{1,0:T(8,128)(2,1)S(1)} collective-permute-done((bf16[2048,128]{1,0:T(8,128)(2,1)}, bf16[2048,128]{1,0:T(8,128)(2,1)S(1)}, u32[]{:S(2)}, u32[]{:S(2)}) %collective-permute-start.10) | collective-permute-done | bytes 524320 | tf_op jit(solution)/shard_map/ppermute | solution.py:270
  96.8 13.5 %collective-permute-done.12.refs_7_ = bf16[2048,128]{1,0:T(8,128)(2,1)S(1)} collective-permute-done((bf16[2048,128]{1,0:T(8,128)(2,1)}, bf16[2048,128]{1,0:T(8,128)(2,1)S(1)}, u32[]{:S(2)}, u32[]{:S(2)}) %collective-permute-start.12) | collective-permute-done | bytes 524320 | tf_op jit(solution)/shard_map/ppermute | solution.py:270
  110.3 17.6 %collective-permute-start.13 = (bf16[2048,128]{1,0:T(8,128)(2,1)S(1)}, bf16[2048,128]{1,0:T(8,128)(2,1)S(1)}, u32[]{:S(2)}, u32[]{:S(2)}) collective-permute-start(bf16[2048,128]{1,0:T(8,128)(2,1)S(1)} %collective-permute-done.12.refs_7_), channel_id=1, source_target_pairs={{0,24},{8,0},{16,8},{24,16},{1,25},{9,1},{17,9},{25,17},{2,26},{10... | collective-permute-start | bytes 1572872 | tf_op jit(solution)/shard_map/ppermute | solution.py:270
  127.9 23.9 %collective-permute-done.11.refs_2_ = bf16[2048,128]{1,0:T(8,128)(2,1)S(1)} collective-permute-done((bf16[2048,128]{1,0:T(8,128)(2,1)S(1)}, bf16[2048,128]{1,0:T(8,128)(2,1)S(1)}, u32[]{:S(2)}, u32[]{:S(2)}) %collective-permute-start.11) | collective-permute-done | bytes 524320 | tf_op jit(solution)/shard_map/ppermute | solution.py:270
  151.8 9.7 %collective-permute-done.13.refs_6_ = bf16[2048,128]{1,0:T(8,128)(2,1)S(1)} collective-permute-done((bf16[2048,128]{1,0:T(8,128)(2,1)S(1)}, bf16[2048,128]{1,0:T(8,128)(2,1)S(1)}, u32[]{:S(2)}, u32[]{:S(2)}) %collective-permute-start.13) | collective-permute-done | bytes 524320 | tf_op jit(solution)/shard_map/ppermute | solution.py:270
  161.5 7.4 collective-permute-start.14
  173.3 9.6 %collective-permute-done.14.refs_1_ = bf16[2048,128]{1,0:T(8,128)(2,1)S(1)} collective-permute-done((bf16[2048,128]{1,0:T(8,128)(2,1)}, bf16[2048,128]{1,0:T(8,128)(2,1)S(1)}, u32[]{:S(2)}, u32[]{:S(2)}) %collective-permute-start.14) | collective-permute-done | bytes 524320 | tf_op jit(solution)/shard_map/ppermute | solution.py:270
  183.9 10.0 %collective-permute-done.17.refs_7_ = bf16[2048,128]{1,0:T(8,128)(2,1)S(1)} collective-permute-done((bf16[2048,128]{1,0:T(8,128)(2,1)}, bf16[2048,128]{1,0:T(8,128)(2,1)S(1)}, u32[]{:S(2)}, u32[]{:S(2)}) %collective-permute-start.17) | collective-permute-done | bytes 524320 | tf_op jit(solution)/shard_map/ppermute | solution.py:270
  204.8 3.8 collective-permute-start.24
  208.6 15.6 %collective-permute-done.18.refs_6_ = bf16[2048,128]{1,0:T(8,128)(2,1)} collective-permute-done((bf16[2048,128]{1,0:T(8,128)(2,1)S(1)}, bf16[2048,128]{1,0:T(8,128)(2,1)}, u32[]{:S(2)}, u32[]{:S(2)}) %collective-permute-start.18) | collective-permute-done | bytes 524320 | tf_op jit(solution)/shard_map/ppermute | solution.py:270
  224.4 24.6 %q_do.3 = (bf16[2048,1024]{1,0:T(8,128)(2,1)}, bf16[2048,1024]{1,0:T(8,128)(2,1)}) custom-call(bf16[2048,2048]{1,0:T(8,128)(2,1)} %get-tuple-element.56.r_ref, bf16[2048,2048]{1,0:T(8,128)(2,1)} %bitcast.70, bf16[2048,4096]{1,0:T(8,128)(2,1)} %all-gather.2.cloned.1.call-done.wq_ref.wo_ref.refs_2_, ...), custom_call_target="tpu_custom_call" | custom-call | flops 17179869184 | bytes 33554432 | tf_op jit(solution)/shard_map/q_do/pallas_call | solution.py:95
  249.1 57.6 %attention.2 = (bf16[2048,2048]{1,0:T(8,128)(2,1)}, bf16[2048,1024]{1,0:T(8,128)(2,1)}, f32[2048,128]{1,0:T(8,128)}, f32[2048,128]{1,0:T(8,128)}, f32[2048,128]{...) custom-call(bf16[2048,1024]{1,0:T(8,128)(2,1)} %get-tuple-element.67, ...), custom_call_target="tpu_custom_call" | custom-call | flops 25769803776 | bytes 20971520 | tf_op jit(solution)/shard_map/attention/pallas_call | solution.py:168
  306.7 24.6 %q_do.2 = (bf16[2048,1024]{1,0:T(8,128)(2,1)}, bf16[2048,1024]{1,0:T(8,128)(2,1)}) custom-call(bf16[2048,2048]{1,0:T(8,128)(2,1)} %get-tuple-element.56.r_ref, bf16[2048,2048]{1,0:T(8,128)(2,1)} %bitcast.71, bf16[2048,4096]{1,0:T(8,128)(2,1)} %all-gather.2.cloned.1.call-done.wq_ref.wo_ref.refs_2_, ...), custom_call_target="tpu_custom_call" | custom-call | flops 17179869184 | bytes 33554432 | tf_op jit(solution)/shard_map/q_do/pallas_call | solution.py:95
  331.4 57.8 %attention.3 = (bf16[2048,2048]{1,0:T(8,128)(2,1)}, bf16[2048,1024]{1,0:T(8,128)(2,1)}, f32[2048,128]{1,0:T(8,128)}, f32[2048,128]{1,0:T(8,128)}, f32[2048,128]{...) custom-call(bf16[2048,1024]{1,0:T(8,128)(2,1)} %get-tuple-element.57, ...), custom_call_target="tpu_custom_call", output_to_operand_aliasing={{0}: (13, {})} | custom-call | flops 25769803776 | bytes 20971520 | tf_op jit(solution)/shard_map/attention/pallas_call | solution.py:168
  389.2 14.6 %fusion.20 = f32[2048,1024]{1,0:T(8,128)} fusion(bf16[2048,2048]{1,0:T(8,128)(2,1)} %get-tuple-element.56.r_ref, bf16[2048,1024]{1,0:T(8,128)(2,1)} %get-tuple-element.72.refs_1_), kind=kOutput, calls=%fused_computation.83 | convolution fusion | flops 8589934592 | bytes 20971520 | tf_op jit(solution)/shard_map/dot_general | solution.py:33
  403.9 14.9 %fusion.19 = f32[2048,1024]{1,0:T(8,128)} fusion(bf16[2048,2048]{1,0:T(8,128)(2,1)} %get-tuple-element.56.r_ref, bf16[2048,1024]{1,0:T(8,128)(2,1)} %get-tuple-element.71.refs_0_), kind=kOutput, calls=%fused_computation.82 | convolution fusion | flops 8589934592 | bytes 20971520 | tf_op jit(solution)/shard_map/dot_general | solution.py:33
  418.9 25.5 %fusion.18 = f32[2048,2048]{1,0:T(8,128)} fusion(bf16[2048,2048]{1,0:T(8,128)(2,1)} %get-tuple-element.70.o_ref, bf16[2048,2048]{1,0:T(8,128)(2,1)} %bitcast.72), kind=kOutput, calls=%fused_computation.81 | convolution fusion | flops 17179869184 | bytes 33554432 | tf_op jit(solution)/shard_map/dot_general | solution.py:33
  448.3 24.2 %collective-permute-done.25 = f32[2048,128]{1,0:T(8,128)S(1)} collective-permute-done((f32[2048,128]{1,0:T(8,128)}, f32[2048,128]{1,0:T(8,128)S(1)}, u32[]{:S(2)}, u32[]{:S(2)}) %collective-permute-start.25) | collective-permute-done | bytes 1048608 | tf_op jit(solution)/shard_map/ppermute | solution.py:270
  472.5 15.3 %collective-permute-done.26 = f32[2048,128]{1,0:T(8,128)S(1)} collective-permute-done((f32[2048,128]{1,0:T(8,128)}, f32[2048,128]{1,0:T(8,128)S(1)}, u32[]{:S(2)}, u32[]{:S(2)}) %collective-permute-start.26) | collective-permute-done | bytes 1048608 | tf_op jit(solution)/shard_map/ppermute | solution.py:270
  488.5 3.5 collective-permute-start.28
  492.0 23.8 %collective-permute-done.27 = f32[2048,128]{1,0:T(8,128)S(1)} collective-permute-done((f32[2048,128]{1,0:T(8,128)S(1)}, f32[2048,128]{1,0:T(8,128)S(1)}, u32[]{:S(2)}, u32[]{:S(2)}) %collective-permute-start.27) | collective-permute-done | bytes 1048608 | tf_op jit(solution)/shard_map/ppermute | solution.py:270
  515.8 18.7 %collective-permute-done.28 = f32[2048,128]{1,0:T(8,128)S(1)} collective-permute-done((f32[2048,128]{1,0:T(8,128)S(1)}, f32[2048,128]{1,0:T(8,128)S(1)}, u32[]{:S(2)}, u32[]{:S(2)}) %collective-permute-start.28) | collective-permute-done | bytes 1048608 | tf_op jit(solution)/shard_map/ppermute | solution.py:270
  536.0 3.7 collective-permute-start.30
  539.8 24.1 %dr_query.1.dr_ref = f32[2048,2048]{1,0:T(8,128)} custom-call(bf16[2048,1024]{1,0:T(8,128)(2,1)} %get-tuple-element.71.refs_0_, bf16[2048,1024]{1,0:T(8,128)(2,1)} %get-tuple-element.72.refs_1_, bf16[2048,4096]{1,0:T(8,128)(2,1)} %all-gather.2.cloned.1.call-done.wq_ref.wo_ref.refs_2_), custom_call_target="tpu_custom_call" | custom-call | flops 17179869184 | bytes 33554432 | tf_op jit(solution)/shard_map/dr_query/pallas_call | solution.py:217
  563.9 18.6 %collective-permute-done.30 = f32[2048,128]{1,0:T(8,128)} collective-permute-done((f32[2048,128]{1,0:T(8,128)}, f32[2048,128]{1,0:T(8,128)}, u32[]{:S(2)}, u32[]{:S(2)}) %collective-permute-start.30) | collective-permute-done | bytes 1048608 | tf_op jit(solution)/shard_map/ppermute | solution.py:270
  586.5 7.2 fusion.10
  597.6 24.2 %collective-permute-done.31 = f32[2048,128]{1,0:T(8,128)S(1)} collective-permute-done((f32[2048,128]{1,0:T(8,128)}, f32[2048,128]{1,0:T(8,128)S(1)}, u32[]{:S(2)}, u32[]{:S(2)}) %collective-permute-start.31) | collective-permute-done | bytes 1048608 | tf_op jit(solution)/shard_map/ppermute | solution.py:270
  621.9 20.1 %collective-permute-done.32 = f32[2048,128]{1,0:T(8,128)S(1)} collective-permute-done((f32[2048,128]{1,0:T(8,128)}, f32[2048,128]{1,0:T(8,128)S(1)}, u32[]{:S(2)}, u32[]{:S(2)}) %collective-permute-start.32) | collective-permute-done | bytes 1048608 | tf_op jit(solution)/shard_map/ppermute | solution.py:270
  645.7 3.5 collective-permute-start.34
  649.2 22.2 %reduce-scatter.23.cloned.1.call-done = f32[256,2048]{1,0:T(8,128)} async-done(((f32[2048,2048]{1,0:T(8,128)}), f32[256,2048]{1,0:T(8,128)}) %reduce-scatter.23.cloned.1.call-update) | async-done | bytes 2097168 | tf_op jit(solution)/shard_map/reduce_scatter | solution.py:306
  671.5 24.3 %out_proj.1 = bf16[2048,2048]{1,0:T(8,128)(2,1)} custom-call(bf16[2048,2048]{1,0:T(8,128)(2,1)} %bitcast.68, bf16[2048,2048]{1,0:T(8,128)(2,1)} %get-tuple-element.70.o_ref, bf16[2048,4096]{1,0:T(8,128)(2,1)} %all-gather.2.cloned.1.call-done.wq_ref.wo_ref.refs_2_), custom_call_target="tpu_custom_call" | custom-call | flops 17179869184 | bytes 33554432 | tf_op jit(solution)/shard_map/out_proj/pallas_call | solution.py:190
  695.7 13.9 %collective-permute-done.34 = f32[2048,128]{1,0:T(8,128)} collective-permute-done((f32[2048,128]{1,0:T(8,128)}, f32[2048,128]{1,0:T(8,128)}, u32[]{:S(2)}, u32[]{:S(2)}) %collective-permute-start.34) | collective-permute-done | bytes 1048608 | tf_op jit(solution)/shard_map/ppermute | solution.py:270
  713.2 3.4 collective-permute-start.36
  716.6 38.1 %collective-permute-done.35 = f32[2048,128]{1,0:T(8,128)S(1)} collective-permute-done((f32[2048,128]{1,0:T(8,128)S(1)}, f32[2048,128]{1,0:T(8,128)S(1)}, u32[]{:S(2)}, u32[]{:S(2)}) %collective-permute-start.35) | collective-permute-done | bytes 1048608 | tf_op jit(solution)/shard_map/ppermute | solution.py:270
  754.7 22.5 %collective-permute-done.36 = f32[2048,128]{1,0:T(8,128)S(1)} collective-permute-done((f32[2048,128]{1,0:T(8,128)S(1)}, f32[2048,128]{1,0:T(8,128)S(1)}, u32[]{:S(2)}, u32[]{:S(2)}) %collective-permute-start.36) | collective-permute-done | bytes 1048608 | tf_op jit(solution)/shard_map/ppermute | solution.py:270
  781.1 4.0 fusion.9
  785.2 24.4 %reduce-scatter.19.cloned.1.call-done = f32[256,256]{1,0:T(8,128)} async-done(((f32[2048,256]{1,0:T(8,128)}), f32[256,256]{1,0:T(8,128)}) %reduce-scatter.19.cloned.1.call-update) | async-done | bytes 262160 | tf_op jit(solution)/shard_map/reduce_scatter | solution.py:306
  809.6 46.5 %reduce-scatter.25.cloned.1.call-done = f32[64,2048]{1,0:T(8,128)} async-done(((f32[256,2048]{1,0:T(8,128)}), f32[64,2048]{1,0:T(8,128)}) %reduce-scatter.25.cloned.1.call-update) | async-done | bytes 524304 | tf_op jit(solution)/shard_map/reduce_scatter | solution.py:309
  858.4 22.9 %norm_back.1 = (bf16[2048,2048]{1,0:T(8,128)(2,1)}, f32[8,2048]{1,0:T(8,128)}) custom-call(bf16[2048,2048]{1,0:T(8,128)(2,1)} %bitcast.69, bf16[2048,2048]{1,0:T(8,128)(2,1)} %bitcast.73, f32[2048,2048]{1,0:T(8,128)} %dr_query.1.dr_ref, bf16[2048,256]{1,0:T(8,128)(2,1)} %pad_maximum_fusion.4.dkv0_ref, bf16[2048,256]{1,0:T(8,128)(2,1)} %pad_maximum_fusion.5.dkv1_ref, ...), custom_call_target="tpu_custom_call" | custom-call | flops 8589934592 | bytes 58720256 | tf_op jit(solution)/shard_map/norm_back/pallas_call | solution.py:254
  896.4 3.4 reduce-scatter.27.cloned.1.call-done
  901.2 20.7 %reduce-scatter.21.cloned.1.call-done = f32[64,256]{1,0:T(8,128)} async-done(((f32[256,256]{1,0:T(8,128)}), f32[64,256]{1,0:T(8,128)}) %reduce-scatter.21.cloned.1.call-update) | async-done | bytes 65552 | tf_op jit(solution)/shard_map/reduce_scatter | solution.py:309
  922.7 19.7 %reduce-scatter.29.cloned.1.call-done = f32[64,256]{1,0:T(8,128)} async-done(((f32[256,256]{1,0:T(8,128)}), f32[64,256]{1,0:T(8,128)}) %reduce-scatter.29.cloned.1.call-update) | async-done | bytes 65552 | tf_op jit(solution)/shard_map/reduce_scatter | solution.py:309
  (202 shorter events, 92.9 us)
Async XLA Ops:
  7.2 217.3 %all-gather.2.cloned.1.call-start = ((), (), s32[]{:S(2)}) async-start(), calls=%async_computation.10 | async-start | bytes 17301504 | tf_op jit(solution)/shard_map/all_gather | solution.py:320
  9.1 530.6 %reduce-scatter.15.cloned.1.call-start = ((), (), s32[]{:S(2)}) async-start(), calls=%async_computation.13 | async-start | bytes 9437184 | tf_op jit(solution)/shard_map/reduce_scatter | solution.py:306
  9.9 5.4 collective-permute-start.5
  13.1 5.4 collective-permute-start
  15.4 8.3 collective-permute-start.6
  19.1 6.9 collective-permute-start.1
  23.7 9.6 %collective-permute-start.7 = (bf16[4,64,512]{2,1,0:T(8,128)(2,1)S(1)}, bf16[4,64,512]{2,1,0:T(8,128)(2,1)S(1)}, u32[]{:S(2)}, u32[]{:S(2)}) collective-permute-start(bf16[4,64,512]{2,1,0:T(8,128)(2,1)S(1)} %bitcast.76), channel_id=1, source_target_pairs={{0,4},{1,5},{2,6},{3,7},{4,0},{5,1},{6,2},{7,3},{8,12},{9,13},{10,... | collective-permute-start | bytes 786440 | tf_op jit(solution)/shard_map/ppermute | solution.py:273
  33.4 11.6 %collective-permute-start.8 = (bf16[2,4,64,512]{3,2,1,0:T(8,128)(2,1)S(1)}, bf16[2,4,64,512]{3,2,1,0:T(8,128)(2,1)S(1)}, u32[]{:S(2)}, u32[]{:S(2)}) collective-permute-start(bf16[2,4,64,512]{3,2,1,0:T(8,128)(2,1)S(1)} %pad_maximum_fusion.6), channel_id=1, source_target_pairs={{0,2},{1,3},{2,0},{3,1},{4,6},{5,7},{6,4},{7,5},{8,10},{9,11},{10,... | collective-permute-start | bytes 1572872 | tf_op jit(solution)/shard_map/ppermute | solution.py:273
  38.6 10.4 %collective-permute-start.3 = (f32[2,4,64]{2,1,0:T(4,128)S(1)}, f32[2,4,64]{2,1,0:T(4,128)S(1)}, u32[]{:S(2)}, u32[]{:S(2)}) collective-permute-start(f32[2,4,64]{2,1,0:T(4,128)S(1)} %pad_maximum_fusion.16), channel_id=1, source_target_pairs={{0,2},{1,3},{2,0},{3,1},{4,6},{5,7},{6,4},{7,5},{8,10},{9,11},{10,... | collective-permute-start | bytes 6152 | tf_op jit(solution)/shard_map/ppermute | solution.py:273
  45.2 7.5 collective-permute-start.9
  67.9 28.9 %collective-permute-start.10 = (bf16[2048,128]{1,0:T(8,128)(2,1)}, bf16[2048,128]{1,0:T(8,128)(2,1)S(1)}, u32[]{:S(2)}, u32[]{:S(2)}) collective-permute-start(bf16[2048,128]{1,0:T(8,128)(2,1)} %get-tuple-element.63.refs_0_), channel_id=1, source_target_pairs={{0,8},{8,16},{16,24},{24,0},{1,9},{9,17},{17,25},{25,1},{2,10},{10... | collective-permute-start | bytes 1572872 | tf_op jit(solution)/shard_map/ppermute | solution.py:270
  70.7 39.6 %collective-permute-start.12 = (bf16[2048,128]{1,0:T(8,128)(2,1)}, bf16[2048,128]{1,0:T(8,128)(2,1)S(1)}, u32[]{:S(2)}, u32[]{:S(2)}) collective-permute-start(bf16[2048,128]{1,0:T(8,128)(2,1)} %get-tuple-element.64.refs_4_), channel_id=1, source_target_pairs={{0,24},{8,0},{16,8},{24,16},{1,25},{9,1},{17,9},{25,17},{2,26},{10... | collective-permute-start | bytes 1572872 | tf_op jit(solution)/shard_map/ppermute | solution.py:270
  96.7 55.1 %collective-permute-start.11 = (bf16[2048,128]{1,0:T(8,128)(2,1)S(1)}, bf16[2048,128]{1,0:T(8,128)(2,1)S(1)}, u32[]{:S(2)}, u32[]{:S(2)}) collective-permute-start(bf16[2048,128]{1,0:T(8,128)(2,1)S(1)} %collective-permute-done.10.refs_1_), channel_id=1, source_target_pairs={{0,8},{8,16},{16,24},{24,0},{1,9},{9,17},{17,25},{25,1},{2,10},{10... | collective-permute-start | bytes 1572872 | tf_op jit(solution)/shard_map/ppermute | solution.py:270
  110.3 51.2 %collective-permute-start.13 = (bf16[2048,128]{1,0:T(8,128)(2,1)S(1)}, bf16[2048,128]{1,0:T(8,128)(2,1)S(1)}, u32[]{:S(2)}, u32[]{:S(2)}) collective-permute-start(bf16[2048,128]{1,0:T(8,128)(2,1)S(1)} %collective-permute-done.12.refs_7_), channel_id=1, source_target_pairs={{0,24},{8,0},{16,8},{24,16},{1,25},{9,1},{17,9},{25,17},{2,26},{10... | collective-permute-start | bytes 1572872 | tf_op jit(solution)/shard_map/ppermute | solution.py:270
  161.5 21.4 %collective-permute-start.14 = (bf16[2048,128]{1,0:T(8,128)(2,1)}, bf16[2048,128]{1,0:T(8,128)(2,1)S(1)}, u32[]{:S(2)}, u32[]{:S(2)}) collective-permute-start(bf16[2048,128]{1,0:T(8,128)(2,1)} %get-tuple-element.65.refs_0_), channel_id=1, source_target_pairs={{0,8},{8,16},{16,24},{24,0},{1,9},{9,17},{17,25},{25,1},{2,10},{10... | collective-permute-start | bytes 1572872 | tf_op jit(solution)/shard_map/ppermute | solution.py:270
  168.9 25.0 %collective-permute-start.17 = (bf16[2048,128]{1,0:T(8,128)(2,1)}, bf16[2048,128]{1,0:T(8,128)(2,1)S(1)}, u32[]{:S(2)}, u32[]{:S(2)}) collective-permute-start(bf16[2048,128]{1,0:T(8,128)(2,1)} %get-tuple-element.66.refs_4_), channel_id=1, source_target_pairs={{0,24},{8,0},{16,8},{24,16},{1,25},{9,1},{17,9},{25,17},{2,26},{10... | collective-permute-start | bytes 1572872 | tf_op jit(solution)/shard_map/ppermute | solution.py:270
  169.9 29.9 %collective-permute-start.22 = (s32[16,128]{1,0:T(8,128)S(1)}, s32[16,128]{1,0:T(8,128)S(1)}, u32[]{:S(2)}, u32[]{:S(2)}) collective-permute-start(s32[16,128]{1,0:T(8,128)S(1)} %copy-done.18), channel_id=1, source_target_pairs={{0,24},{8,0},{16,8},{24,16},{1,25},{9,1},{17,9},{25,17},{2,26},{10... | collective-permute-start | bytes 24584 | tf_op jit(solution)/shard_map/ppermute | solution.py:270
  171.9 29.8 %collective-permute-start.21 = (s32[16,128]{1,0:T(8,128)S(1)}, s32[16,128]{1,0:T(8,128)S(1)}, u32[]{:S(2)}, u32[]{:S(2)}) collective-permute-start(s32[16,128]{1,0:T(8,128)S(1)} %copy-done.18), channel_id=1, source_target_pairs={{0,16},{8,24},{16,0},{24,8},{1,17},{9,25},{17,1},{25,9},{2,18},{10... | collective-permute-start | bytes 24584 | tf_op jit(solution)/shard_map/ppermute | solution.py:270
  172.4 29.3 %collective-permute-start.20 = (s32[16,128]{1,0:T(8,128)S(1)}, s32[16,128]{1,0:T(8,128)S(1)}, u32[]{:S(2)}, u32[]{:S(2)}) collective-permute-start(s32[16,128]{1,0:T(8,128)S(1)} %copy-done.18), channel_id=1, source_target_pairs={{0,8},{8,16},{16,24},{24,0},{1,9},{9,17},{17,25},{25,1},{2,10},{10... | collective-permute-start | bytes 24584 | tf_op jit(solution)/shard_map/ppermute | solution.py:270
  182.9 25.7 %collective-permute-start.15 = (bf16[2048,128]{1,0:T(8,128)(2,1)S(1)}, bf16[2048,128]{1,0:T(8,128)(2,1)}, u32[]{:S(2)}, u32[]{:S(2)}) collective-permute-start(bf16[2048,128]{1,0:T(8,128)(2,1)S(1)} %collective-permute-done.14.refs_1_), channel_id=1, source_target_pairs={{0,8},{8,16},{16,24},{24,0},{1,9},{9,17},{17,25},{25,1},{2,10},{10... | collective-permute-start | bytes 1572872 | tf_op jit(solution)/shard_map/ppermute | solution.py:270
  193.9 30.3 %collective-permute-start.18 = (bf16[2048,128]{1,0:T(8,128)(2,1)S(1)}, bf16[2048,128]{1,0:T(8,128)(2,1)}, u32[]{:S(2)}, u32[]{:S(2)}) collective-permute-start(bf16[2048,128]{1,0:T(8,128)(2,1)S(1)} %collective-permute-done.17.refs_7_), channel_id=1, source_target_pairs={{0,24},{8,0},{16,8},{24,16},{1,25},{9,1},{17,9},{25,17},{2,26},{10... | collective-permute-start | bytes 1572872 | tf_op jit(solution)/shard_map/ppermute | solution.py:270
  204.8 44.3 %collective-permute-start.23 = (bf16[2048,128]{1,0:T(8,128)(2,1)S(1)}, bf16[2048,128]{1,0:T(8,128)(2,1)}, u32[]{:S(2)}, u32[]{:S(2)}) collective-permute-start(bf16[2048,128]{1,0:T(8,128)(2,1)S(1)} %collective-permute-done.11.refs_2_), channel_id=1, source_target_pairs={{0,8},{8,16},{16,24},{24,0},{1,9},{9,17},{17,25},{25,1},{2,10},{10... | collective-permute-start | bytes 1572872 | tf_op jit(solution)/shard_map/ppermute | solution.py:270
  204.8 44.3 %collective-permute-start.24 = (bf16[2048,128]{1,0:T(8,128)(2,1)S(1)}, bf16[2048,128]{1,0:T(8,128)(2,1)}, u32[]{:S(2)}, u32[]{:S(2)}) collective-permute-start(bf16[2048,128]{1,0:T(8,128)(2,1)S(1)} %collective-permute-done.13.refs_6_), channel_id=1, source_target_pairs={{0,24},{8,0},{16,8},{24,16},{1,25},{9,1},{17,9},{25,17},{2,26},{10... | collective-permute-start | bytes 1572872 | tf_op jit(solution)/shard_map/ppermute | solution.py:270
  208.6 122.7 %collective-permute-start.16 = (bf16[2048,128]{1,0:T(8,128)(2,1)}, bf16[2048,128]{1,0:T(8,128)(2,1)}, u32[]{:S(2)}, u32[]{:S(2)}) collective-permute-start(bf16[2048,128]{1,0:T(8,128)(2,1)} %collective-permute-done.15.refs_2_), channel_id=1, source_target_pairs={{0,8},{8,16},{16,24},{24,0},{1,9},{9,17},{17,25},{25,1},{2,10},{10... | collective-permute-start | bytes 1572872 | tf_op jit(solution)/shard_map/ppermute | solution.py:270
  224.3 107.1 %collective-permute-start.19 = (bf16[2048,128]{1,0:T(8,128)(2,1)}, bf16[2048,128]{1,0:T(8,128)(2,1)}, u32[]{:S(2)}, u32[]{:S(2)}) collective-permute-start(bf16[2048,128]{1,0:T(8,128)(2,1)} %collective-permute-done.18.refs_6_), channel_id=1, source_target_pairs={{0,24},{8,0},{16,8},{24,16},{1,25},{9,1},{17,9},{25,17},{2,26},{10... | collective-permute-start | bytes 1572872 | tf_op jit(solution)/shard_map/ppermute | solution.py:270
  403.9 178.8 %reduce-scatter.11.cloned.1.call-start = ((), (), s32[]{:S(2)}) async-start(), calls=%async_computation.11 | async-start | bytes 9437184 | tf_op jit(solution)/shard_map/reduce_scatter | solution.py:306
  418.8 252.6 %reduce-scatter.23.cloned.1.call-start = ((), (), s32[]{:S(2)}) async-start(), calls=%async_computation.17 | async-start | bytes 18874368 | tf_op jit(solution)/shard_map/reduce_scatter | solution.py:306
  444.4 340.8 %reduce-scatter.17.cloned.1.call-start = ((), (), s32[]{:S(2)}) async-start(), calls=%async_computation.14 | async-start | bytes 1310720 | tf_op jit(solution)/shard_map/reduce_scatter | solution.py:309
  444.4 28.1 %collective-permute-start.25 = (f32[2048,128]{1,0:T(8,128)}, f32[2048,128]{1,0:T(8,128)S(1)}, u32[]{:S(2)}, u32[]{:S(2)}) collective-permute-start(f32[2048,128]{1,0:T(8,128)} %get-tuple-element.73), channel_id=1, source_target_pairs={{0,8},{8,16},{16,24},{24,0},{1,9},{9,17},{17,25},{25,1},{2,10},{10... | collective-permute-start | bytes 3145736 | tf_op jit(solution)/shard_map/ppermute | solution.py:270
  446.4 41.4 %collective-permute-start.26 = (f32[2048,128]{1,0:T(8,128)}, f32[2048,128]{1,0:T(8,128)S(1)}, u32[]{:S(2)}, u32[]{:S(2)}) collective-permute-start(f32[2048,128]{1,0:T(8,128)} %get-tuple-element.74), channel_id=1, source_target_pairs={{0,24},{8,0},{16,8},{24,16},{1,25},{9,1},{17,9},{25,17},{2,26},{10... | collective-permute-start | bytes 3145736 | tf_op jit(solution)/shard_map/ppermute | solution.py:270
  487.9 27.9 %collective-permute-start.27 = (f32[2048,128]{1,0:T(8,128)S(1)}, f32[2048,128]{1,0:T(8,128)S(1)}, u32[]{:S(2)}, u32[]{:S(2)}) collective-permute-start(f32[2048,128]{1,0:T(8,128)S(1)} %add.71), channel_id=1, source_target_pairs={{0,8},{8,16},{16,24},{24,0},{1,9},{9,17},{17,25},{25,1},{2,10},{10... | collective-permute-start | bytes 3145736 | tf_op jit(solution)/shard_map/ppermute | solution.py:270
  488.5 46.1 %collective-permute-start.28 = (f32[2048,128]{1,0:T(8,128)S(1)}, f32[2048,128]{1,0:T(8,128)S(1)}, u32[]{:S(2)}, u32[]{:S(2)}) collective-permute-start(f32[2048,128]{1,0:T(8,128)S(1)} %add.72), channel_id=1, source_target_pairs={{0,24},{8,0},{16,8},{24,16},{1,25},{9,1},{17,9},{25,17},{2,26},{10... | collective-permute-start | bytes 3145736 | tf_op jit(solution)/shard_map/ppermute | solution.py:270
  534.7 29.2 %collective-permute-start.29 = (f32[2048,128]{1,0:T(8,128)S(1)}, f32[2048,128]{1,0:T(8,128)S(1)}, u32[]{:S(2)}, u32[]{:S(2)}) collective-permute-start(f32[2048,128]{1,0:T(8,128)S(1)} %add.73), channel_id=1, source_target_pairs={{0,8},{8,16},{16,24},{24,0},{1,9},{9,17},{17,25},{25,1},{2,10},{10... | collective-permute-start | bytes 3145736 | tf_op jit(solution)/shard_map/ppermute | solution.py:270
  536.0 46.5 %collective-permute-start.30 = (f32[2048,128]{1,0:T(8,128)}, f32[2048,128]{1,0:T(8,128)}, u32[]{:S(2)}, u32[]{:S(2)}) collective-permute-start(f32[2048,128]{1,0:T(8,128)} %add.74), channel_id=1, source_target_pairs={{0,24},{8,0},{16,8},{24,16},{1,25},{9,1},{17,9},{25,17},{2,26},{10... | collective-permute-start | bytes 3145736 | tf_op jit(solution)/shard_map/ppermute | solution.py:270
  539.7 245.4 %reduce-scatter.13.cloned.1.call-start = ((), (), s32[]{:S(2)}) async-start(), calls=%async_computation.12 | async-start | bytes 1310720 | tf_op jit(solution)/shard_map/reduce_scatter | solution.py:309
  582.7 226.9 %reduce-scatter.19.cloned.1.call-start = ((), (), s32[]{:S(2)}) async-start(), calls=%async_computation.15 | async-start | bytes 2359296 | tf_op jit(solution)/shard_map/reduce_scatter | solution.py:306
  593.7 262.4 %reduce-scatter.25.cloned.1.call-start = ((), (), s32[]{:S(2)}) async-start(), calls=%async_computation.18 | async-start | bytes 2621440 | tf_op jit(solution)/shard_map/reduce_scatter | solution.py:309
  593.8 28.1 %collective-permute-start.31 = (f32[2048,128]{1,0:T(8,128)}, f32[2048,128]{1,0:T(8,128)S(1)}, u32[]{:S(2)}, u32[]{:S(2)}) collective-permute-start(f32[2048,128]{1,0:T(8,128)} %get-tuple-element.87), channel_id=1, source_target_pairs={{0,8},{8,16},{16,24},{24,0},{1,9},{9,17},{17,25},{25,1},{2,10},{10... | collective-permute-start | bytes 3145736 | tf_op jit(solution)/shard_map/ppermute | solution.py:270
  594.5 47.5 %collective-permute-start.32 = (f32[2048,128]{1,0:T(8,128)}, f32[2048,128]{1,0:T(8,128)S(1)}, u32[]{:S(2)}, u32[]{:S(2)}) collective-permute-start(f32[2048,128]{1,0:T(8,128)} %get-tuple-element.88), channel_id=1, source_target_pairs={{0,24},{8,0},{16,8},{24,16},{1,25},{9,1},{17,9},{25,17},{2,26},{10... | collective-permute-start | bytes 3145736 | tf_op jit(solution)/shard_map/ppermute | solution.py:270
  644.3 51.4 %collective-permute-start.33 = (f32[2048,128]{1,0:T(8,128)}, f32[2048,128]{1,0:T(8,128)}, u32[]{:S(2)}, u32[]{:S(2)}) collective-permute-start(f32[2048,128]{1,0:T(8,128)} %add.77), channel_id=1, source_target_pairs={{0,8},{8,16},{16,24},{24,0},{1,9},{9,17},{17,25},{25,1},{2,10},{10... | collective-permute-start | bytes 3145736 | tf_op jit(solution)/shard_map/ppermute | solution.py:270
  645.7 63.9 %collective-permute-start.34 = (f32[2048,128]{1,0:T(8,128)}, f32[2048,128]{1,0:T(8,128)}, u32[]{:S(2)}, u32[]{:S(2)}) collective-permute-start(f32[2048,128]{1,0:T(8,128)} %add.78), channel_id=1, source_target_pairs={{0,24},{8,0},{16,8},{24,16},{1,25},{9,1},{17,9},{25,17},{2,26},{10... | collective-permute-start | bytes 3145736 | tf_op jit(solution)/shard_map/ppermute | solution.py:270
  671.4 228.4 %reduce-scatter.27.cloned.1.call-start = ((), (), s32[]{:S(2)}) async-start(), calls=%async_computation.19 | async-start | bytes 2359296 | tf_op jit(solution)/shard_map/reduce_scatter | solution.py:306
  711.4 43.3 %collective-permute-start.35 = (f32[2048,128]{1,0:T(8,128)S(1)}, f32[2048,128]{1,0:T(8,128)S(1)}, u32[]{:S(2)}, u32[]{:S(2)}) collective-permute-start(f32[2048,128]{1,0:T(8,128)S(1)} %add.79), channel_id=1, source_target_pairs={{0,8},{8,16},{16,24},{24,0},{1,9},{9,17},{17,25},{25,1},{2,10},{10... | collective-permute-start | bytes 3145736 | tf_op jit(solution)/shard_map/ppermute | solution.py:270
  713.2 64.0 %collective-permute-start.36 = (f32[2048,128]{1,0:T(8,128)S(1)}, f32[2048,128]{1,0:T(8,128)S(1)}, u32[]{:S(2)}, u32[]{:S(2)}) collective-permute-start(f32[2048,128]{1,0:T(8,128)S(1)} %add.80), channel_id=1, source_target_pairs={{0,24},{8,0},{16,8},{24,16},{1,25},{9,1},{17,9},{25,17},{2,26},{10... | collective-permute-start | bytes 3145736 | tf_op jit(solution)/shard_map/ppermute | solution.py:270
  856.1 65.8 %reduce-scatter.21.cloned.1.call-start = ((), (), s32[]{:S(2)}) async-start(), calls=%async_computation.16 | async-start | bytes 327680 | tf_op jit(solution)/shard_map/reduce_scatter | solution.py:309
  891.0 51.5 %reduce-scatter.29.cloned.1.call-start = ((), (), s32[]{:S(2)}) async-start(), calls=%async_computation.20 | async-start | bytes 327680 | tf_op jit(solution)/shard_map/reduce_scatter | solution.py:309
  891.0 4.5 collective-permute-start.40
  895.6 4.2 collective-permute-start.41
  (32 other events, 1484.0 us)
Sparse Core Ops, SparseCore 0:
  11.5 156.9 all-gather.1
  404.0 72.7 reduce-scatter.14
  480.2 71.4 reduce-scatter.10
  555.2 116.1 reduce-scatter.22
  673.5 36.5 reduce-scatter.16
  712.2 52.4 reduce-scatter.12
  768.0 41.5 reduce-scatter.18
  812.4 43.6 reduce-scatter.24
  859.4 40.3 reduce-scatter.26
  901.9 19.9 reduce-scatter.20
  924.2 18.2 reduce-scatter.28
